TPU v7x, 128 devices: a whole 4x4x4 slice. The times are simulated.
128 devices in a mesh: leaf: 16 (over x, z), sub: 8 (over y, core).
Axes of the slice: x: 4, y: 4, z: 4, core: 2. Of those that a mesh axis runs over, the one named last changes fastest.
Arguments:
- vectors: bfloat16 [64, 655360], P(None, ('leaf', 'sub')), may hold values from -6 to 6
- row_counts: int32 [128], replicated, may hold values from 3072 to 5120, as said below
- tree_slot: int32 [655360], P(('leaf', 'sub')), may hold values from -1 to 524287, as said below
- leaf_inverse: bfloat16 [2048, 256, 256], P(('leaf', 'sub')), may hold values from -0.375 to 0.375
- left_basis: bfloat16 [11, 32, 524288], P(None, None, ('leaf', 'sub')), may hold values from -0.41992188 to 0.41992188
- right_basis: bfloat16 [11, 32, 524288], P(None, None, ('leaf', 'sub')), may hold values from -6 to 6
Outputs:
- applied: bfloat16 [64, 655360], P(None, ('leaf', 'sub'))
Inputs may be any that keep to these rules, and one draw needn't show every extreme that they name: The first row_counts[d] of the 5120 slots of owner d are live; the counts sum to 524288. `tree_slot`: live slots hold distinct tree positions covering 0 .. 524287, dead slots hold -1. Tree owner t holds positions t*4096 .. (t+1)*4096 - 1; the live rows of one mesh owner go to one tree owner at most 40 at a time.
All inputs are finite; a program needn't handle non-finite values.
Results may differ from a plain program's by a relative error of at most 0.014.
Values may be sent and summed in bfloat16 or wider, within the bound.
A program may use at most 64 MiB of HBM per device.

v0:
```python
import functools
import math

import jax
import jax.numpy as jnp
from jax import lax
from jax.experimental import pallas as pl
from jax.experimental.pallas import tpu as pltpu
from jax.sharding import PartitionSpec as P

DEV = 128
PEER = 40
HALF = 20
BLOCK = 24
ROWS = 4096
SLOTS = 5120
VECS = 64
LEAF = 256
RANK = 32
LOCAL = 4
CROSS = 7
F32 = jnp.float32
BF16 = jnp.bfloat16
I32 = jnp.int32
VMEM = pl.BlockSpec(memory_space=pltpu.VMEM)
SMEM = pl.BlockSpec(memory_space=pltpu.SMEM)
NT = (((1,), (1,)), ((), ()))
MESH = pl.DeviceIdType.MESH


def my_index():
    return lax.axis_index("leaf") * 8 + lax.axis_index("sub")


def iota(shape, dim):
    return lax.broadcasted_iota(I32, shape, dim)


def dot_nt(a, b):
    return lax.dot_general(a, b, NT, preferred_element_type=F32)


def dot(a, b):
    return jnp.dot(a, b, preferred_element_type=F32)


def bucket_row(owner, rank):
    return jnp.where(rank < HALF, owner * BLOCK + rank, DEV * BLOCK + owner * BLOCK + rank - HALF)


def live_slots(counts, slots):
    place = iota((40, 128), 0) * 128 + iota((40, 128), 1)
    return (place < counts[my_index()]) & (slots >= 0)


def route(counts, slots_ref, rank_ref):
    slots = slots_ref[...]
    live = live_slots(counts, slots)
    owner = jnp.where(live, slots >> 12, DEV)
    high = ((slots & 4095) >> 6).astype(F32)
    low = (slots & 63).astype(F32)
    ids = iota((DEV, 128), 0)
    before = jnp.where(iota((128, 256), 0) < iota((128, 256), 1), 1.0, 0.0).astype(BF16)
    base = jnp.zeros((DEV, 128), F32)
    for a in range(40):
        hit = ids == owner[a : a + 1, :]
        earlier = dot(jnp.where(hit, 1.0, 0.0).astype(BF16), before)
        rank_ref[a : a + 1, :] = jnp.sum(jnp.where(hit, base + earlier[:, :128], 0.0), axis=0, keepdims=True)
        base = base + earlier[:, 128:]
    ranks = rank_ref[...].astype(I32)
    r64 = iota((64, 128), 0)
    lane = iota((64, 128), 1).astype(F32)
    total = jnp.zeros((DEV, 256), F32)
    for a in range(40):
        hit = jnp.where(ids == owner[a : a + 1, :], 1.0, 0.0).astype(BF16)
        match = r64 == ranks[a : a + 1, :]
        table = jnp.concatenate(
            [
                jnp.where(match, float(a), 0.0),
                jnp.where(match, lane, 0.0),
                jnp.where(match, high[a : a + 1, :], 0.0),
                jnp.where(match, low[a : a + 1, :], 0.0),
            ],
            axis=0,
        ).astype(BF16)
        total = total + dot_nt(hit, table)
    return live, owner, ranks, base, total


def device(index):
    return {"leaf": index // 8, "sub": lax.rem(index, 8)}


def enter():
    me = my_index()
    barrier = pltpu.get_barrier_semaphore()

    def signal(i, carry):
        pl.semaphore_signal(barrier, 1, device_id=device(lax.rem(me + i, DEV)), device_id_type=MESH)
        return carry

    lax.fori_loop(1, DEV, signal, 0)


def entered():
    pl.semaphore_wait(pltpu.get_barrier_semaphore(), DEV - 1)


def send_block(src, dst, t, send_sem, recv_sem):
    me = my_index()

    @pl.when(t != me)
    def _():
        pltpu.make_async_remote_copy(
            src_ref=src.at[t],
            dst_ref=dst.at[me],
            send_sem=send_sem,
            recv_sem=recv_sem.at[me],
            device_id=device(t),
            device_id_type=MESH,
        ).start()

    @pl.when(t == me)
    def _():
        pltpu.make_async_copy(src.at[t], dst.at[t], recv_sem.at[t]).start()


def sent(src, send_sem):
    whole = src.at[pl.ds(0, DEV - 1)]
    pltpu.make_async_copy(whole, whole, send_sem).wait()


def gather_and_send(pick, x, stage, src, dst, send_sem, recv_sem):
    left = iota((1, 128), 1) < VECS
    me = my_index()

    def some(c, carry):
        ts = [lax.rem(me + 1 + c * 4 + u, DEV) for u in range(4)]
        for u, t in enumerate(ts):
            for r in range(HALF):
                one = x[pl.ds(pick[t, r], 1), :]
                two = x[pl.ds(pick[t, r + HALF], 1), :]
                stage[u, r : r + 1, :] = jnp.where(left, one, two)
            for r in range(HALF, HALF + 2):
                stage[u, r : r + 1, :] = x[pl.ds(SLOTS + (r - HALF) * DEV + t, 1), :]
            src[t] = stage[u].astype(BF16)
        for t in ts:
            send_block(src, dst, t, send_sem, recv_sem)
        return carry

    lax.fori_loop(0, DEV // 4, some, 0)


def receive(arrived, recv_sem, y):
    me = my_index()

    def some(c, carry):
        for u in range(4):
            t = lax.rem(me + 2 * DEV - 1 - c * 4 - u, DEV)
            pltpu.make_async_copy(arrived.at[t], arrived.at[t], recv_sem.at[t]).wait()
            rows = arrived[t].astype(F32)
            at = pl.multiple_of(t * BLOCK, 8)
            y[pl.ds(at, BLOCK), :] = rows
            y[pl.ds(pl.multiple_of(DEV * BLOCK + at, 8), BLOCK), :] = pltpu.roll(rows, 64, 1)
        return carry

    lax.fori_loop(0, DEV // 4, some, 0)


def block(k):
    return slice((CROSS - 1 - k) * RANK, (CROSS - k) * RANK)


def above(k):
    return slice(0, (CROSS - 1 - k) * RANK)


def rows_of(j):
    return slice((5 - j) * RANK, (6 - j) * RANK)


def place():
    leaf, sub = lax.axis_index("leaf"), lax.axis_index("sub")
    return leaf // 4, lax.rem(leaf, 4), sub // 2, lax.rem(sub, 2)


def group(phase):
    x, z, y, core = place()
    leaf, sub = lax.axis_index("leaf"), lax.axis_index("sub")
    return [
        (2, core, lambda c: {"leaf": leaf, "sub": y * 2 + c}),
        (4, y, lambda c: {"leaf": leaf, "sub": c * 2 + core}),
        (4, z, lambda c: {"leaf": x * 4 + c, "sub": sub}),
        (4, x, lambda c: {"leaf": c * 4 + z, "sub": sub}),
    ][phase]


def share(phase, buf, send_sem, recv_sem, wait=False):
    members, me, target = group(phase)
    for i in range(1, members):
        other = lax.rem(me + i, members)
        copy = pltpu.make_async_remote_copy(
            src_ref=buf.at[me],
            dst_ref=buf.at[me],
            send_sem=send_sem.at[phase, i],
            recv_sem=recv_sem.at[phase, me],
            device_id=target(other),
            device_id_type=MESH,
        )
        if wait:
            copy.wait_send()
            pltpu.make_async_copy(buf.at[other], buf.at[other], recv_sem.at[phase, other]).wait()
        else:
            copy.start()


def kernel(
    counts,
    slots_ref,
    vec,
    inverse_h,
    left_h,
    right_h,
    out,
    inverse,
    left,
    right,
    pick_v,
    pick,
    rank_ref,
    flat_v,
    flat,
    x,
    stage,
    src1,
    dst1,
    src2,
    dst2,
    y,
    inv_v,
    inv,
    back_v,
    back,
    field,
    v_a,
    v_b,
    v_c,
    v_d,
    g_a,
    g_b,
    g_c,
    g_d,
    partner,
    load_sem,
    index_sem,
    send_sem,
    recv1,
    recv2,
    send_v,
    recv_v,
    send_g,
    recv_g,
):
    scale = [1.0 / math.sqrt(ROWS * 2**k) for k in range(CROSS)]
    with jax.named_scope("enter"):
        loads = [
            pltpu.make_async_copy(h, v, load_sem.at[i])
            for i, (h, v) in enumerate(((left_h, left), (right_h, right), (inverse_h, inverse)))
        ]
        for load in loads:
            load.start()
        enter()
    with jax.named_scope("route"):
        live, owner, ranks, base, total = route(counts, slots_ref, rank_ref)
        flat_v[...] = jnp.clip(jnp.where(live, bucket_row(owner, ranks), 0), 0, 2 * DEV * BLOCK - 1)
        both = total[:, :128].astype(I32)
        source = both * 128 + pltpu.roll(both, 64, 1)
        lane128 = iota((DEV, 128), 1)
        pick_v[...] = jnp.clip(jnp.where(lane128 < PEER, source, 0), 0, SLOTS - 1)
        pick_copy = pltpu.make_async_copy(pick_v, pick, index_sem.at[0])
        pick_copy.start()
        flat_copy = pltpu.make_async_copy(flat_v, flat, index_sem.at[1])
        flat_copy.start()
        position = total[:, 128:]
        x[SLOTS : SLOTS + DEV, :] = jnp.where(lane128.astype(F32) < base, position, 64.0)
        x[SLOTS + DEV :, :] = pltpu.roll(position, 64, 1)
    with jax.named_scope("rows"):
        for a in range(40):
            part = vec[:, a * 128 : (a + 1) * 128].astype(F32)
            x[a * 128 : (a + 1) * 128, :] = jnp.concatenate([part, part], axis=0).T
        for u in range(4):
            stage[u] = jnp.zeros((BLOCK, 128), F32)
        pick_copy.wait()
    with jax.named_scope("entered"):
        entered()
    with jax.named_scope("send"):
        gather_and_send(pick, x, stage, src1, dst1, send_sem.at[0], recv1)
    with jax.named_scope("gram"):
        loads[0].wait()
        loads[1].wait()
        gram = jnp.zeros((CROSS * RANK - RANK, CROSS * RANK), F32)
        for c in range(4):
            at = slice(c * 1024, (c + 1) * 1024)
            gram = gram + dot_nt(
                left[LOCAL : LOCAL + 6, :, at].reshape(6 * RANK, 1024),
                right[LOCAL:, :, at].reshape(CROSS * RANK, 1024),
            )
        core = group(0)[1]
        g_a[core] = jnp.zeros((192, 256), BF16)
        for j in range(CROSS - 1):
            for k in range(j + 1, CROSS):
                g_a[core, rows_of(j), block(k)] = gram[
                    j * RANK : (j + 1) * RANK, k * RANK : (k + 1) * RANK
                ].astype(BF16)
        share(0, g_a, send_g, recv_g)
    with jax.named_scope("receive"):
        receive(dst1, recv1, y)
    with jax.named_scope("inv"):
        high = y[pl.ds(20, DEV, stride=BLOCK), :]
        low = y[pl.ds(21, DEV, stride=BLOCK), :]
        spot = high.astype(I32) * 64 + low.astype(I32)
        back_v[...] = jnp.clip(jnp.where(lane128 < PEER, spot, 0), 0, ROWS - 1)
        back_copy = pltpu.make_async_copy(back_v, back, index_sem.at[2])
        back_copy.start()
        high_t = high.T
        low_t = low.T
        ids = iota((64, 128), 0).astype(F32)
        lanes = iota((64, 128), 1).astype(F32)
        found = jnp.zeros((64, 128), F32)
        for r in range(PEER):
            hit = jnp.where(ids == high_t[r : r + 1, :], 1.0, 0.0).astype(BF16)
            match = ids == low_t[r : r + 1, :]
            table = jnp.concatenate(
                [jnp.where(match, lanes, 0.0), jnp.where(match, float(r), 0.0)], axis=0
            ).astype(BF16)
            found = found + dot_nt(hit, table)
        whole = found.astype(I32)
        inv_v[...] = jnp.clip(
            jnp.where(iota((64, 128), 1) < 64, bucket_row(whole, pltpu.roll(whole, 64, 1)), 0),
            0,
            2 * DEV * BLOCK - 1,
        )
        inv_copy = pltpu.make_async_copy(inv_v, inv, index_sem.at[3])
        inv_copy.start()
    with jax.named_scope("gram_y"):
        share(0, g_a, send_g, recv_g, wait=True)
        ysum = g_a[0].astype(F32) + g_a[1].astype(F32)
        g_b[group(1)[1]] = ysum[:160].astype(BF16)
        share(1, g_b, send_g, recv_g)
        inv_copy.wait()
    with jax.named_scope("tree"):

        def some(c, carry):
            for u in range(128):
                x[pl.ds(c * 128 + u, 1), :] = y[pl.ds(inv[c * 2 + u // 64, u % 64], 1), :]
            return carry

        lax.fori_loop(0, ROWS // 128, some, 0)
    with jax.named_scope("leaf"):
        loads[2].wait()

        def leaf(l, carry):
            at = pl.multiple_of(l * LEAF, LEAF)
            rows = x[pl.ds(at, LEAF), :].T[:VECS].astype(BF16)
            field[:, pl.ds(at, LEAF)] = dot_nt(rows, inverse[l])
            return carry

        lax.fori_loop(0, ROWS // LEAF, leaf, 0)
    with jax.named_scope("gram_z"):
        share(1, g_b, send_g, recv_g, wait=True)
        zsum = (g_b[0, :96, :128].astype(F32) + g_b[1, :96, :128].astype(F32)) + (
            g_b[2, :96, :128].astype(F32) + g_b[3, :96, :128].astype(F32)
        )
        g_c[group(2)[1]] = zsum.astype(BF16)
        share(2, g_c, send_g, recv_g)
    with jax.named_scope("local"):
        for level in range(LOCAL):
            size = LEAF * 2**level
            nodes = ROWS // size

            def pair(m, carry):
                at = [pl.multiple_of(m * 2 * size, size), pl.multiple_of(m * 2 * size + size, size)]
                coeff = [
                    (
                        dot_nt(field[:, pl.ds(s, size)].astype(BF16), right[level, :, pl.ds(s, size)])
                        * (1.0 / math.sqrt(size))
                    ).astype(BF16)
                    for s in at
                ]
                for n in range(2):
                    field[:, pl.ds(at[n], size)] -= dot(coeff[1 - n], left[level, :, pl.ds(at[n], size)])
                return carry

            lax.fori_loop(0, nodes // 2, pair, 0, unroll=True)
    with jax.named_scope("gram_x"):
        share(2, g_c, send_g, recv_g, wait=True)
        xsum = (g_c[0, :32].astype(F32) + g_c[1, :32].astype(F32)) + (
            g_c[2, :32].astype(F32) + g_c[3, :32].astype(F32)
        )
        g_d[group(3)[1]] = xsum.astype(BF16)
        share(3, g_d, send_g, recv_g)
    with jax.named_scope("reduce"):
        v = jnp.zeros((VECS, CROSS * RANK), F32)
        for c in range(4):
            at = slice(c * 1024, (c + 1) * 1024)
            v = v + dot_nt(field[:, at].astype(BF16), right[LOCAL:, :, at].reshape(CROSS * RANK, 1024))

    def merge(k, va, vb, ga, gb):
        pa = (vb[:, block(k)] * scale[k]).astype(BF16)
        pb = (va[:, block(k)] * scale[k]).astype(BF16)
        if k == CROSS - 1:
            return pa, pb, None
        p2 = jnp.concatenate([pa, pb], axis=1)
        g2 = jnp.concatenate([ga[rows_of(k), above(k)], gb[rows_of(k), above(k)]], axis=0).astype(BF16)
        return pa, pb, va[:, above(k)] + vb[:, above(k)] - dot(p2, g2)

    def keep(k, p):
        partner[:, k * RANK : (k + 1) * RANK] = p

    with jax.named_scope("cross_core"):
        core = group(0)[1]
        v_a[core] = jnp.zeros((VECS, 256), F32)
        for k in range(CROSS):
            v_a[core, :, block(k)] = v[:, k * RANK : (k + 1) * RANK]
        share(0, v_a, send_v, recv_v)
        share(0, v_a, send_v, recv_v, wait=True)
        pa, pb, v = merge(0, v_a[0], v_a[1], g_a[0], g_a[1])
        keep(0, jnp.where(core == 0, pa, pb))

    def four(phase, k, v, v_buf, g_buf):
        me = group(phase)[1]
        width = v_buf.shape[2]
        v_buf[me] = jnp.concatenate([v, jnp.zeros((VECS, width), F32)], axis=1)[:, :width].astype(BF16)
        share(phase, v_buf, send_v, recv_v)
        share(phase, v_buf, send_v, recv_v, wait=True)
        vs = [v_buf[i].astype(F32) for i in range(4)]
        gs = [g_buf[i].astype(F32) for i in range(4)]
        p0, p1, v01 = merge(k, vs[0], vs[1], gs[0], gs[1])
        p2, p3, v23 = merge(k, vs[2], vs[3], gs[2], gs[3])
        keep(k, jnp.where(me < 2, jnp.where(me == 0, p0, p1), jnp.where(me == 2, p2, p3)))
        pa, pb, v = merge(k + 1, v01, v23, gs[0] + gs[1], gs[2] + gs[3])
        keep(k + 1, jnp.where(me < 2, pa, pb))
        return v

    with jax.named_scope("cross_y"):
        v = four(1, 1, v, v_b, g_b)
    with jax.named_scope("cross_z"):
        v = four(2, 3, v, v_c, g_c)
    with jax.named_scope("cross_x"):
        share(3, g_d, send_g, recv_g, wait=True)
        four(3, 5, v, v_d, g_d)
    with jax.named_scope("finish"):
        for c in range(16):
            at = slice(c * LEAF, (c + 1) * LEAF)
            done = field[:, at] - dot(
                partner[:, : CROSS * RANK], left[LOCAL:, :, at].reshape(CROSS * RANK, LEAF)
            )
            x[at, :] = jnp.concatenate([done, done], axis=0).T
        back_copy.wait()
        sent(src1, send_sem.at[0])
    with jax.named_scope("send_back"):
        gather_and_send(back, x, stage, src2, dst2, send_sem.at[1], recv2)
    with jax.named_scope("receive_back"):
        flat_copy.wait()
        receive(dst2, recv2, y)
    with jax.named_scope("output"):
        alive = jnp.where(live_slots(counts, slots_ref[...]), 1, 0)

        def pull(c, carry):
            for u in range(128):
                x[pl.ds(c * 128 + u, 1), :] = y[pl.ds(flat[c, u], 1), :]
            return carry

        lax.fori_loop(0, 40, pull, 0)
        for a in range(40):
            part = x[a * 128 : (a + 1) * 128, :].T[:VECS]
            out[:, a * 128 : (a + 1) * 128] = jnp.where(alive[a : a + 1, :] > 0, part, 0.0).astype(BF16)
        sent(src2, send_sem.at[1])


def body(vectors, row_counts, tree_slot, leaf_inverse, left_basis, right_basis):
    anywhere = pl.BlockSpec(memory_space=pl.ANY)
    dma = pltpu.SemaphoreType.DMA
    blocks = pltpu.VMEM((DEV, BLOCK, 128), BF16)
    return pl.pallas_call(
        kernel,
        out_shape=jax.ShapeDtypeStruct((VECS, SLOTS), BF16),
        in_specs=[SMEM, VMEM, VMEM, anywhere, anywhere, anywhere],
        out_specs=VMEM,
        scratch_shapes=[
            pltpu.VMEM(leaf_inverse.shape, BF16),
            pltpu.VMEM(left_basis.shape, BF16),
            pltpu.VMEM(right_basis.shape, BF16),
            pltpu.VMEM((DEV, 128), I32),
            pltpu.SMEM((DEV, 128), I32),
            pltpu.VMEM((40, 128), F32),
            pltpu.VMEM((40, 128), I32),
            pltpu.SMEM((40, 128), I32),
            pltpu.VMEM((SLOTS + 2 * DEV, 128), F32),
            pltpu.VMEM((4, BLOCK, 128), F32),
            blocks,
            blocks,
            blocks,
            blocks,
            pltpu.VMEM((2 * DEV * BLOCK, 128), F32),
            pltpu.VMEM((64, 128), I32),
            pltpu.SMEM((64, 128), I32),
            pltpu.VMEM((DEV, 128), I32),
            pltpu.SMEM((DEV, 128), I32),
            pltpu.VMEM((VECS, ROWS), F32),
            pltpu.VMEM((2, VECS, 256), F32),
            pltpu.VMEM((4, VECS, 256), BF16),
            pltpu.VMEM((4, VECS, 128), BF16),
            pltpu.VMEM((4, VECS, 128), BF16),
            pltpu.VMEM((2, 192, 256), BF16),
            pltpu.VMEM((4, 160, 256), BF16),
            pltpu.VMEM((4, 96, 128), BF16),
            pltpu.VMEM((4, 32, 128), BF16),
            pltpu.VMEM((VECS, 256), BF16),
            dma((3,)),
            dma((4,)),
            dma((2,)),
            dma((DEV,)),
            dma((DEV,)),
            dma((4, 4)),
            dma((4, 4)),
            dma((4, 4)),
            dma((4, 4)),
        ],
        compiler_params=pltpu.CompilerParams(collective_id=0, has_side_effects=True),
        name="apply",
    )(row_counts, tree_slot.reshape(40, 128), vectors, leaf_inverse, left_basis, right_basis)


def solution(mesh):
    both = ("leaf", "sub")
    return jax.shard_map(
        body,
        mesh=mesh,
        in_specs=(
            P(None, both),
            P(),
            P(both),
            P(both, None, None),
            P(None, None, both),
            P(None, None, both),
        ),
        out_specs=P(None, both),
        check_vma=False,
    )
```

profile of v0, /device:TPU:1, one launch (start us, length us, event | category | flops | bytes accessed | tf_op | source)
XLA Modules:
  0.0 88.4 jit_solution(18064260227596033469)
XLA Ops:
  0.0 86.4 %apply.1 = bf16[64,5120]{1,0:T(8,128)(2,1)} custom-call(s32[128]{0:T(128)} %counts.1, s32[40,128]{1,0:T(8,128)} %bitcast.1, bf16[64,5120]{1,0:T(8,128)(2,1)} %vec.1, bf16[16,256,256]{2,1,0:T(8,128)(2,1)} %inverse_h.1, bf16[11,32,4096]{2,1,0:T(8,128)(2,1)} %left_h.1, bf16[11,32,4096]{2,1,0:T(8,128)(2,1)} %right_h.1), custom_call_target="tpu_custom_call" | custom-call | tf_op jit(solution)/shard_map/apply/pallas_call | solution.py:485
  86.4 2.0 %copy.8 = bf16[64,5120]{1,0:T(8,128)(2,1)} copy(bf16[64,5120]{1,0:T(8,128)(2,1)} %apply.1) | data formatting | bytes 1310720
where the time goes:
time: 88.5 us; the launch traced here: 88.4 us
  Pallas kernels  86.4 us (98%)
  local copies, waits for them, and re-layouts  1.97 us (2%)
    pallas_call x1, Pallas kernels, body(): pl.pallas_call(kernel, out_shape=jax.ShapeDtypeStruct((VECS, SLOTS), BF16...  86.4 us
    unnamed x1, local copies, waits for them, and re-layouts  1.97 us

commit v1 on v0

--- a/solution.py
+++ b/solution.py
@@ -87,6 +87,39 @@
     return live, owner, ranks, base, total
 
 
+def far_first():
+    def hops(c):
+        return sum(min(d, 4 - d) for d in c)
+
+    chips = [(i * 29 % 64 // 16, i * 29 % 16 // 4, i * 29 % 4) for i in range(64)]
+    chips.sort(key=lambda c: -hops(c))
+    codes = [c[0] + 4 * c[1] + 16 * c[2] for c in chips]
+    return [sum(codes[4 * w + j] * 64**j for j in range(4)) for w in range(16)]
+
+
+WORDS = far_first()
+
+
+def word_at(c):
+    word = WORDS[0]
+    for w in range(1, 16):
+        word = jnp.where(c == w, WORDS[w], word)
+    return word
+
+
+def peers(word, sign):
+    x, z, y, core = place()
+    found = []
+    for j in range(4):
+        code = word // 64**j % 64
+        px = lax.rem(x + 4 + sign * (code % 4), 4)
+        py = lax.rem(y + 4 + sign * (code // 4 % 4), 4)
+        pz = lax.rem(z + 4 + sign * (code // 16), 4)
+        for pc in (1 - core, core):
+            found.append((px * 4 + pz, py * 2 + pc))
+    return found
+
+
 def device(index):
     return {"leaf": index // 8, "sub": lax.rem(index, 8)}
 
@@ -95,34 +128,12 @@
     me = my_index()
     barrier = pltpu.get_barrier_semaphore()
 
-    def signal(i, carry):
+    for i in range(1, DEV):
         pl.semaphore_signal(barrier, 1, device_id=device(lax.rem(me + i, DEV)), device_id_type=MESH)
-        return carry
-
-    lax.fori_loop(1, DEV, signal, 0)
 
 
 def entered():
     pl.semaphore_wait(pltpu.get_barrier_semaphore(), DEV - 1)
-
-
-def send_block(src, dst, t, send_sem, recv_sem):
-    me = my_index()
-
-    @pl.when(t != me)
-    def _():
-        pltpu.make_async_remote_copy(
-            src_ref=src.at[t],
-            dst_ref=dst.at[me],
-            send_sem=send_sem,
-            recv_sem=recv_sem.at[me],
-            device_id=device(t),
-            device_id_type=MESH,
-        ).start()
-
-    @pl.when(t == me)
-    def _():
-        pltpu.make_async_copy(src.at[t], dst.at[t], recv_sem.at[t]).start()
 
 
 def sent(src, send_sem):
@@ -134,37 +145,57 @@
     left = iota((1, 128), 1) < VECS
     me = my_index()
 
-    def some(c, carry):
-        ts = [lax.rem(me + 1 + c * 4 + u, DEV) for u in range(4)]
-        for u, t in enumerate(ts):
+    def fill(word):
+        for u, (leaf, sub) in enumerate(peers(word, 1)):
+            t = leaf * 8 + sub
             for r in range(HALF):
                 one = x[pl.ds(pick[t, r], 1), :]
                 two = x[pl.ds(pick[t, r + HALF], 1), :]
                 stage[u, r : r + 1, :] = jnp.where(left, one, two)
             for r in range(HALF, HALF + 2):
                 stage[u, r : r + 1, :] = x[pl.ds(SLOTS + (r - HALF) * DEV + t, 1), :]
-            src[t] = stage[u].astype(BF16)
+        for u, (leaf, sub) in enumerate(peers(word, 1)):
+            src[leaf * 8 + sub] = stage[u].astype(BF16)
+
+    def send(word, last=False):
+        for u, (leaf, sub) in enumerate(peers(word, 1)):
+            t = leaf * 8 + sub
+            if last and u == 7:
+                pltpu.make_async_copy(src.at[me], dst.at[me], recv_sem.at[me]).start()
+                continue
+            pltpu.make_async_remote_copy(
+                src_ref=src.at[t],
+                dst_ref=dst.at[me],
+                send_sem=send_sem,
+                recv_sem=recv_sem.at[me],
+                device_id={"leaf": leaf, "sub": sub},
+                device_id_type=MESH,
+            ).start()
+
+    fill(WORDS[0])
+
+    def loop(c, carry):
+        send(word_at(c))
+        fill(word_at(c + 1))
+        return carry
+
+    lax.fori_loop(0, 15, loop, 0)
+    send(WORDS[15], True)
+
+
+def receive(arrived, recv_sem, y):
+    def some(c, carry):
+        ts = [leaf * 8 + sub for leaf, sub in peers(word_at(c), -1)]
         for t in ts:
-            send_block(src, dst, t, send_sem, recv_sem)
-        return carry
-
-    lax.fori_loop(0, DEV // 4, some, 0)
-
-
-def receive(arrived, recv_sem, y):
-    me = my_index()
-
-    def some(c, carry):
-        for u in range(4):
-            t = lax.rem(me + 2 * DEV - 1 - c * 4 - u, DEV)
             pltpu.make_async_copy(arrived.at[t], arrived.at[t], recv_sem.at[t]).wait()
+        for t in ts:
             rows = arrived[t].astype(F32)
             at = pl.multiple_of(t * BLOCK, 8)
             y[pl.ds(at, BLOCK), :] = rows
             y[pl.ds(pl.multiple_of(DEV * BLOCK + at, 8), BLOCK), :] = pltpu.roll(rows, 64, 1)
         return carry
 
-    lax.fori_loop(0, DEV // 4, some, 0)
+    lax.fori_loop(0, 16, some, 0)
 
 
 def block(k):
@@ -188,39 +219,67 @@
     x, z, y, core = place()
     leaf, sub = lax.axis_index("leaf"), lax.axis_index("sub")
     return [
-        (2, core, lambda c: {"leaf": leaf, "sub": y * 2 + c}),
-        (4, y, lambda c: {"leaf": leaf, "sub": c * 2 + core}),
-        (4, z, lambda c: {"leaf": x * 4 + c, "sub": sub}),
-        (4, x, lambda c: {"leaf": c * 4 + z, "sub": sub}),
+        (2, core, None),
+        (4, y, lambda m, c: {"leaf": leaf, "sub": m * 2 + c}),
+        (4, z, lambda m, c: {"leaf": x * 4 + m, "sub": y * 2 + c}),
+        (4, x, lambda m, c: {"leaf": m * 4 + z, "sub": y * 2 + c}),
     ][phase]
 
 
 def share(phase, buf, send_sem, recv_sem, wait=False):
     members, me, target = group(phase)
-    for i in range(1, members):
-        other = lax.rem(me + i, members)
-        copy = pltpu.make_async_remote_copy(
+    leaf, (x, z, y, core) = lax.axis_index("leaf"), place()
+
+    def copy_to(i, c, to):
+        return pltpu.make_async_remote_copy(
             src_ref=buf.at[me],
             dst_ref=buf.at[me],
-            send_sem=send_sem.at[phase, i],
+            send_sem=send_sem.at[phase, 2 * i + c],
             recv_sem=recv_sem.at[phase, me],
-            device_id=target(other),
+            device_id=to,
             device_id_type=MESH,
         )
+
+    def act(copy):
         if wait:
             copy.wait_send()
-            pltpu.make_async_copy(buf.at[other], buf.at[other], recv_sem.at[phase, other]).wait()
         else:
             copy.start()
 
+    if phase == 0:
+        act(copy_to(1, 0, {"leaf": leaf, "sub": y * 2 + 1 - core}))
+    else:
+
+        @pl.when(core == 1)
+        def _():
+            for i in (2, 1, 3):
+                for c in range(2):
+                    act(copy_to(i, c, target(lax.rem(me + i, members), c)))
+
+    if wait:
+        for i in range(1, members):
+            other = lax.rem(me + i, members)
+            pltpu.make_async_copy(buf.at[other], buf.at[other], recv_sem.at[phase, other]).wait()
+
+
+def fold(a):
+    return jnp.concatenate([a[:32], a[32:]], axis=1)
+
+
+def unfold(a):
+    return jnp.concatenate([a[:, :64], a[:, 64:]], axis=0)
+
 
 def kernel(
     counts,
-    slots_ref,
-    vec,
+    slots_h,
+    vec_h,
     inverse_h,
     left_h,
     right_h,
+    out_h,
+    slots_ref,
+    vec,
     out,
     inverse,
     left,
@@ -265,12 +324,21 @@
     with jax.named_scope("enter"):
         loads = [
             pltpu.make_async_copy(h, v, load_sem.at[i])
-            for i, (h, v) in enumerate(((left_h, left), (right_h, right), (inverse_h, inverse)))
+            for i, (h, v) in enumerate(
+                (
+                    (slots_h, slots_ref),
+                    (vec_h, vec),
+                    (left_h, left),
+                    (right_h, right),
+                    (inverse_h, inverse),
+                )
+            )
         ]
         for load in loads:
             load.start()
         enter()
     with jax.named_scope("route"):
+        loads[0].wait()
         live, owner, ranks, base, total = route(counts, slots_ref, rank_ref)
         flat_v[...] = jnp.clip(jnp.where(live, bucket_row(owner, ranks), 0), 0, 2 * DEV * BLOCK - 1)
         both = total[:, :128].astype(I32)
@@ -285,10 +353,11 @@
         x[SLOTS : SLOTS + DEV, :] = jnp.where(lane128.astype(F32) < base, position, 64.0)
         x[SLOTS + DEV :, :] = pltpu.roll(position, 64, 1)
     with jax.named_scope("rows"):
+        loads[1].wait()
         for a in range(40):
             part = vec[:, a * 128 : (a + 1) * 128].astype(F32)
             x[a * 128 : (a + 1) * 128, :] = jnp.concatenate([part, part], axis=0).T
-        for u in range(4):
+        for u in range(8):
             stage[u] = jnp.zeros((BLOCK, 128), F32)
         pick_copy.wait()
     with jax.named_scope("entered"):
@@ -296,8 +365,8 @@
     with jax.named_scope("send"):
         gather_and_send(pick, x, stage, src1, dst1, send_sem.at[0], recv1)
     with jax.named_scope("gram"):
-        loads[0].wait()
-        loads[1].wait()
+        loads[2].wait()
+        loads[3].wait()
         gram = jnp.zeros((CROSS * RANK - RANK, CROSS * RANK), F32)
         for c in range(4):
             at = slice(c * 1024, (c + 1) * 1024)
@@ -313,6 +382,12 @@
                     j * RANK : (j + 1) * RANK, k * RANK : (k + 1) * RANK
                 ].astype(BF16)
         share(0, g_a, send_g, recv_g)
+    with jax.named_scope("gram_y"):
+        share(0, g_a, send_g, recv_g, wait=True)
+        ysum = g_a[0].astype(F32) + g_a[1].astype(F32)
+        mine = group(1)[1]
+        g_b[mine, :160] = ysum[:160, :128].astype(BF16)
+        g_b[mine, 160:] = ysum[128:160, 128:].astype(BF16)
     with jax.named_scope("receive"):
         receive(dst1, recv1, y)
     with jax.named_scope("inv"):
@@ -342,10 +417,6 @@
         )
         inv_copy = pltpu.make_async_copy(inv_v, inv, index_sem.at[3])
         inv_copy.start()
-    with jax.named_scope("gram_y"):
-        share(0, g_a, send_g, recv_g, wait=True)
-        ysum = g_a[0].astype(F32) + g_a[1].astype(F32)
-        g_b[group(1)[1]] = ysum[:160].astype(BF16)
         share(1, g_b, send_g, recv_g)
         inv_copy.wait()
     with jax.named_scope("tree"):
@@ -357,15 +428,10 @@
 
         lax.fori_loop(0, ROWS // 128, some, 0)
     with jax.named_scope("leaf"):
-        loads[2].wait()
-
-        def leaf(l, carry):
-            at = pl.multiple_of(l * LEAF, LEAF)
-            rows = x[pl.ds(at, LEAF), :].T[:VECS].astype(BF16)
-            field[:, pl.ds(at, LEAF)] = dot_nt(rows, inverse[l])
-            return carry
-
-        lax.fori_loop(0, ROWS // LEAF, leaf, 0)
+        loads[4].wait()
+        for l in range(ROWS // LEAF):
+            at = slice(l * LEAF, (l + 1) * LEAF)
+            field[:, at] = dot_nt(x[at, :].T[:VECS].astype(BF16), inverse[l])
     with jax.named_scope("gram_z"):
         share(1, g_b, send_g, recv_g, wait=True)
         zsum = (g_b[0, :96, :128].astype(F32) + g_b[1, :96, :128].astype(F32)) + (
@@ -405,13 +471,18 @@
             at = slice(c * 1024, (c + 1) * 1024)
             v = v + dot_nt(field[:, at].astype(BF16), right[LOCAL:, :, at].reshape(CROSS * RANK, 1024))
 
+    def level_rows(k, g):
+        if k == 1:
+            return jnp.concatenate([g[128:160], g[160:]], axis=1)[:, above(1)]
+        return g[rows_of(k), above(k)]
+
     def merge(k, va, vb, ga, gb):
         pa = (vb[:, block(k)] * scale[k]).astype(BF16)
         pb = (va[:, block(k)] * scale[k]).astype(BF16)
         if k == CROSS - 1:
             return pa, pb, None
         p2 = jnp.concatenate([pa, pb], axis=1)
-        g2 = jnp.concatenate([ga[rows_of(k), above(k)], gb[rows_of(k), above(k)]], axis=0).astype(BF16)
+        g2 = jnp.concatenate([level_rows(k, ga), level_rows(k, gb)], axis=0).astype(BF16)
         return pa, pb, va[:, above(k)] + vb[:, above(k)] - dot(p2, g2)
 
     def keep(k, p):
@@ -429,11 +500,21 @@
 
     def four(phase, k, v, v_buf, g_buf):
         me = group(phase)[1]
-        width = v_buf.shape[2]
-        v_buf[me] = jnp.concatenate([v, jnp.zeros((VECS, width), F32)], axis=1)[:, :width].astype(BF16)
+        v = v.astype(BF16).astype(F32)
+        if phase == 1:
+            v_buf[me, :64] = v[:, :128].astype(BF16)
+            v_buf[me, 64:] = fold(v[:, 128:]).astype(BF16)
+        elif phase == 2:
+            v_buf[me] = v.astype(BF16)
+        else:
+            v_buf[me] = fold(v).astype(BF16)
         share(phase, v_buf, send_v, recv_v)
         share(phase, v_buf, send_v, recv_v, wait=True)
         vs = [v_buf[i].astype(F32) for i in range(4)]
+        if phase == 1:
+            vs = [jnp.concatenate([u[:64], unfold(u[64:])], axis=1) for u in vs]
+        elif phase == 3:
+            vs = [unfold(u) for u in vs]
         gs = [g_buf[i].astype(F32) for i in range(4)]
         p0, p1, v01 = merge(k, vs[0], vs[1], gs[0], gs[1])
         p2, p3, v23 = merge(k, vs[2], vs[3], gs[2], gs[3])
@@ -466,15 +547,28 @@
     with jax.named_scope("output"):
         alive = jnp.where(live_slots(counts, slots_ref[...]), 1, 0)
 
-        def pull(c, carry):
+        def pull(c):
             for u in range(128):
-                x[pl.ds(c * 128 + u, 1), :] = y[pl.ds(flat[c, u], 1), :]
+                x[pl.ds(pl.multiple_of(c * 128, 128) + u, 1), :] = y[pl.ds(flat[c, u], 1), :]
+
+        def push(a):
+            at = pl.multiple_of(a * 128, 128)
+            part = x[pl.ds(at, 128), :].T[:VECS]
+            out[:, pl.ds(at, 128)] = jnp.where(slots_ref[pl.ds(a, 1), :] > 0, part, 0.0).astype(BF16)
+
+        slots_ref[...] = alive
+        pull(0)
+
+        def step(c, carry):
+            pull(c + 1)
+            push(c)
             return carry
 
-        lax.fori_loop(0, 40, pull, 0)
-        for a in range(40):
-            part = x[a * 128 : (a + 1) * 128, :].T[:VECS]
-            out[:, a * 128 : (a + 1) * 128] = jnp.where(alive[a : a + 1, :] > 0, part, 0.0).astype(BF16)
+        lax.fori_loop(0, 39, step, 0)
+        push(39)
+        store = pltpu.make_async_copy(out, out_h, load_sem.at[0])
+        store.start()
+        store.wait()
         sent(src2, send_sem.at[1])
 
 
@@ -485,9 +579,12 @@
     return pl.pallas_call(
         kernel,
         out_shape=jax.ShapeDtypeStruct((VECS, SLOTS), BF16),
-        in_specs=[SMEM, VMEM, VMEM, anywhere, anywhere, anywhere],
-        out_specs=VMEM,
+        in_specs=[SMEM] + [anywhere] * 5,
+        out_specs=anywhere,
         scratch_shapes=[
+            pltpu.VMEM((40, 128), I32),
+            pltpu.VMEM((VECS, SLOTS), BF16),
+            pltpu.VMEM((VECS, SLOTS), BF16),
             pltpu.VMEM(leaf_inverse.shape, BF16),
             pltpu.VMEM(left_basis.shape, BF16),
             pltpu.VMEM(right_basis.shape, BF16),
@@ -497,7 +594,7 @@
             pltpu.VMEM((40, 128), I32),
             pltpu.SMEM((40, 128), I32),
             pltpu.VMEM((SLOTS + 2 * DEV, 128), F32),
-            pltpu.VMEM((4, BLOCK, 128), F32),
+            pltpu.VMEM((8, BLOCK, 128), F32),
             blocks,
             blocks,
             blocks,
@@ -509,22 +606,22 @@
             pltpu.SMEM((DEV, 128), I32),
             pltpu.VMEM((VECS, ROWS), F32),
             pltpu.VMEM((2, VECS, 256), F32),
-            pltpu.VMEM((4, VECS, 256), BF16),
+            pltpu.VMEM((4, 96, 128), BF16),
             pltpu.VMEM((4, VECS, 128), BF16),
-            pltpu.VMEM((4, VECS, 128), BF16),
+            pltpu.VMEM((4, 32, 128), BF16),
             pltpu.VMEM((2, 192, 256), BF16),
-            pltpu.VMEM((4, 160, 256), BF16),
+            pltpu.VMEM((4, 192, 128), BF16),
             pltpu.VMEM((4, 96, 128), BF16),
             pltpu.VMEM((4, 32, 128), BF16),
             pltpu.VMEM((VECS, 256), BF16),
-            dma((3,)),
+            dma((5,)),
             dma((4,)),
             dma((2,)),
             dma((DEV,)),
             dma((DEV,)),
+            dma((4, 8)),
             dma((4, 4)),
-            dma((4, 4)),
-            dma((4, 4)),
+            dma((4, 8)),
             dma((4, 4)),
         ],
         compiler_params=pltpu.CompilerParams(collective_id=0, has_side_effects=True),

time: 88.5 us -> 74.6 us (0.84)
  Pallas kernels: 86.4 us -> 72.5 us
    pallas_call x1, Pallas kernels: 86.4 us -> 72.5 us  [body(): pl.pallas_call(kernel, out_shape=jax.ShapeDtypeStruct((VECS, SLOTS), BF16...]
where the time goes in v1:
time: 74.6 us; the launch traced here: 74.4 us
  Pallas kernels  72.5 us (97%)
  local copies, waits for them, and re-layouts  1.97 us (3%)
    pallas_call x1, Pallas kernels, body(): pl.pallas_call(kernel, out_shape=jax.ShapeDtypeStruct((VECS, SLOTS), BF16...  72.5 us
    unnamed x1, local copies, waits for them, and re-layouts  1.97 us

profile of v1, /device:TPU:1, one launch (start us, length us, event | category | flops | bytes accessed | tf_op | source)
XLA Modules:
  0.0 74.4 jit_solution(9803426166238917043)
XLA Ops:
  0.0 72.5 %apply.1 = bf16[64,5120]{1,0:T(8,128)(2,1)} custom-call(s32[128]{0:T(128)} %counts.1, s32[40,128]{1,0:T(8,128)} %bitcast.1, bf16[64,5120]{1,0:T(8,128)(2,1)} %vec_h.1, bf16[16,256,256]{2,1,0:T(8,128)(2,1)} %inverse_h.1, bf16[11,32,4096]{2,1,0:T(8,128)(2,1)} %left_h.1, bf16[11,32,4096]{2,1,0:T(8,128)(2,1)} %right_h.1), custom_call_target="tpu_custom_call" | custom-call | tf_op jit(solution)/shard_map/apply/pallas_call | solution.py:579
  72.5 2.0 %copy.8 = bf16[64,5120]{1,0:T(8,128)(2,1)} copy(bf16[64,5120]{1,0:T(8,128)(2,1)} %apply.1) | data formatting | bytes 1310720

commit v2 on v1

--- a/solution.py
+++ b/solution.py
@@ -3,6 +3,7 @@
 
 import jax
 import jax.numpy as jnp
+import numpy as np
 from jax import lax
 from jax.experimental import pallas as pl
 from jax.experimental.pallas import tpu as pltpu
@@ -11,7 +12,7 @@
 DEV = 128
 PEER = 40
 HALF = 20
-BLOCK = 24
+BLOCK = 20
 ROWS = 4096
 SLOTS = 5120
 VECS = 64
@@ -28,8 +29,36 @@
 MESH = pl.DeviceIdType.MESH
 
 
-def my_index():
-    return lax.axis_index("leaf") * 8 + lax.axis_index("sub")
+FAR = (2, 1, 3, 0)
+PAIRS = sorted(((dx, dz) for dx in FAR for dz in FAR), key=lambda c: -sum(min(d, 4 - d) for d in c))
+ORDER = [(dx, dy, dz, dc) for dx, dz in PAIRS for dy in FAR for dc in (1, 0)]
+CODES = np.array([32 * dx + 8 * dz + 2 * dy + dc for dx, dy, dz, dc in ORDER], np.int32).reshape(16, 8).T.reshape(-1)
+
+
+def place():
+    leaf, sub = lax.axis_index("leaf"), lax.axis_index("sub")
+    return leaf // 4, lax.rem(leaf, 4), sub // 2, lax.rem(sub, 2)
+
+
+def wrapped(at, d):
+    return lax.rem(at + 4 + d, 4)
+
+
+def chosen(n, values):
+    value = values[0]
+    for k in range(1, len(values)):
+        value = jnp.where(n == k, values[k], value)
+    return value
+
+
+def group_of(c, sign):
+    x, z, y, core = place()
+    if isinstance(c, int):
+        dx, dz = PAIRS[c]
+    else:
+        dx, dz = chosen(c, [p[0] for p in PAIRS]), chosen(c, [p[1] for p in PAIRS])
+    leaf = wrapped(x, sign * dx) * 4 + wrapped(z, sign * dz)
+    return [{"leaf": leaf, "sub": wrapped(y, sign * dy) * 2 + pc} for dy in FAR for pc in (1 - core, core)]
 
 
 def iota(shape, dim):
@@ -44,30 +73,41 @@
     return jnp.dot(a, b, preferred_element_type=F32)
 
 
-def bucket_row(owner, rank):
+def bucket_row(label, rank):
+    owner = (label & 15) * 8 + (label >> 4)
     return jnp.where(rank < HALF, owner * BLOCK + rank, DEV * BLOCK + owner * BLOCK + rank - HALF)
 
 
 def live_slots(counts, slots):
-    place = iota((40, 128), 0) * 128 + iota((40, 128), 1)
-    return (place < counts[my_index()]) & (slots >= 0)
-
-
-def route(counts, slots_ref, rank_ref):
+    index = iota((40, 128), 0) * 128 + iota((40, 128), 1)
+    mine = lax.axis_index("leaf") * 8 + lax.axis_index("sub")
+    return (index < counts[mine]) & (slots >= 0)
+
+
+def route(counts, slots_ref, codes, rank_ref):
     slots = slots_ref[...]
     live = live_slots(counts, slots)
-    owner = jnp.where(live, slots >> 12, DEV)
+    x, z, y, core = place()
+    away = (
+        (((slots >> 17) + 4 - x) & 3) * 32
+        + (((slots >> 15) + 4 - z) & 3) * 8
+        + (((slots >> 13) + 4 - y) & 3) * 2
+        + (((slots >> 12) + 2 - core) & 1)
+    )
+    owner = jnp.where(live, away, DEV)
     high = ((slots & 4095) >> 6).astype(F32)
     low = (slots & 63).astype(F32)
-    ids = iota((DEV, 128), 0)
+    ids = codes[...]
     before = jnp.where(iota((128, 256), 0) < iota((128, 256), 1), 1.0, 0.0).astype(BF16)
-    base = jnp.zeros((DEV, 128), F32)
+    start = (iota((DEV, 128), 0) * 64).astype(F32)
+    base = start
     for a in range(40):
         hit = ids == owner[a : a + 1, :]
         earlier = dot(jnp.where(hit, 1.0, 0.0).astype(BF16), before)
         rank_ref[a : a + 1, :] = jnp.sum(jnp.where(hit, base + earlier[:, :128], 0.0), axis=0, keepdims=True)
         base = base + earlier[:, 128:]
-    ranks = rank_ref[...].astype(I32)
+    found = rank_ref[...].astype(I32)
+    ranks = found & 63
     r64 = iota((64, 128), 0)
     lane = iota((64, 128), 1).astype(F32)
     total = jnp.zeros((DEV, 256), F32)
@@ -84,118 +124,75 @@
             axis=0,
         ).astype(BF16)
         total = total + dot_nt(hit, table)
-    return live, owner, ranks, base, total
-
-
-def far_first():
-    def hops(c):
-        return sum(min(d, 4 - d) for d in c)
-
-    chips = [(i * 29 % 64 // 16, i * 29 % 16 // 4, i * 29 % 4) for i in range(64)]
-    chips.sort(key=lambda c: -hops(c))
-    codes = [c[0] + 4 * c[1] + 16 * c[2] for c in chips]
-    return [sum(codes[4 * w + j] * 64**j for j in range(4)) for w in range(16)]
-
-
-WORDS = far_first()
-
-
-def word_at(c):
-    word = WORDS[0]
-    for w in range(1, 16):
-        word = jnp.where(c == w, WORDS[w], word)
-    return word
-
-
-def peers(word, sign):
-    x, z, y, core = place()
-    found = []
-    for j in range(4):
-        code = word // 64**j % 64
-        px = lax.rem(x + 4 + sign * (code % 4), 4)
-        py = lax.rem(y + 4 + sign * (code // 4 % 4), 4)
-        pz = lax.rem(z + 4 + sign * (code // 16), 4)
-        for pc in (1 - core, core):
-            found.append((px * 4 + pz, py * 2 + pc))
-    return found
-
-
-def device(index):
-    return {"leaf": index // 8, "sub": lax.rem(index, 8)}
+    return live, found >> 6, ranks, base - start, total
 
 
 def enter():
-    me = my_index()
     barrier = pltpu.get_barrier_semaphore()
-
-    for i in range(1, DEV):
-        pl.semaphore_signal(barrier, 1, device_id=device(lax.rem(me + i, DEV)), device_id_type=MESH)
+    for c in range(16):
+        for to in group_of(c, 1)[: 8 if c < 15 else 7]:
+            pl.semaphore_signal(barrier, 1, device_id=to, device_id_type=MESH)
 
 
 def entered():
     pl.semaphore_wait(pltpu.get_barrier_semaphore(), DEV - 1)
 
 
+def await_bytes(part, sem):
+    pltpu.make_async_copy(part, part, sem).wait()
+
+
 def sent(src, send_sem):
-    whole = src.at[pl.ds(0, DEV - 1)]
-    pltpu.make_async_copy(whole, whole, send_sem).wait()
-
-
-def gather_and_send(pick, x, stage, src, dst, send_sem, recv_sem):
+    await_bytes(src.at[pl.ds(0, 5 * (DEV - 1))], send_sem)
+
+
+def remote(src, dst, send_sem, recv_sem, to):
+    return pltpu.make_async_remote_copy(
+        src_ref=src, dst_ref=dst, send_sem=send_sem, recv_sem=recv_sem, device_id=to, device_id_type=MESH
+    )
+
+
+def gather_and_send(pick, x, stage, src, dst, send_sem, recv_sem, sign):
     left = iota((1, 128), 1) < VECS
-    me = my_index()
-
-    def fill(word):
-        for u, (leaf, sub) in enumerate(peers(word, 1)):
-            t = leaf * 8 + sub
+
+    def fill(c):
+        for u in range(8):
             for r in range(HALF):
-                one = x[pl.ds(pick[t, r], 1), :]
-                two = x[pl.ds(pick[t, r + HALF], 1), :]
+                one = x[pl.ds(pick.at[r, pl.ds(16 * u, 16)][c], 1), :]
+                two = x[pl.ds(pick.at[r + HALF, pl.ds(16 * u, 16)][c], 1), :]
                 stage[u, r : r + 1, :] = jnp.where(left, one, two)
-            for r in range(HALF, HALF + 2):
-                stage[u, r : r + 1, :] = x[pl.ds(SLOTS + (r - HALF) * DEV + t, 1), :]
-        for u, (leaf, sub) in enumerate(peers(word, 1)):
-            src[leaf * 8 + sub] = stage[u].astype(BF16)
-
-    def send(word, last=False):
-        for u, (leaf, sub) in enumerate(peers(word, 1)):
-            t = leaf * 8 + sub
-            if last and u == 7:
-                pltpu.make_async_copy(src.at[me], dst.at[me], recv_sem.at[me]).start()
-                continue
-            pltpu.make_async_remote_copy(
-                src_ref=src.at[t],
-                dst_ref=dst.at[me],
-                send_sem=send_sem,
-                recv_sem=recv_sem.at[me],
-                device_id={"leaf": leaf, "sub": sub},
-                device_id_type=MESH,
-            ).start()
-
-    fill(WORDS[0])
+            for q in range(5):
+                src[(c * 8 + u) * 5 + q] = stage[u, 4 * q : 4 * q + 4, :].astype(BF16)
+
+    def send(c):
+        for u, to in enumerate(group_of(c, sign)):
+            i = c * 8 + u
+            part = pl.ds(i * 5, 5)
+            if isinstance(c, int) and i == DEV - 1:
+                pltpu.make_async_copy(src.at[part], dst.at[part], recv_sem.at[c]).start()
+            else:
+                remote(src.at[part], dst.at[part], send_sem, recv_sem.at[c], to).start()
+
+    fill(0)
 
     def loop(c, carry):
-        send(word_at(c))
-        fill(word_at(c + 1))
+        send(c)
+        fill(c + 1)
         return carry
 
     lax.fori_loop(0, 15, loop, 0)
-    send(WORDS[15], True)
+    send(15)
 
 
 def receive(arrived, recv_sem, y):
-    def some(c, carry):
-        ts = [leaf * 8 + sub for leaf, sub in peers(word_at(c), -1)]
-        for t in ts:
-            pltpu.make_async_copy(arrived.at[t], arrived.at[t], recv_sem.at[t]).wait()
-        for t in ts:
-            rows = arrived[t].astype(F32)
-            at = pl.multiple_of(t * BLOCK, 8)
-            y[pl.ds(at, BLOCK), :] = rows
-            y[pl.ds(pl.multiple_of(DEV * BLOCK + at, 8), BLOCK), :] = pltpu.roll(rows, 64, 1)
-        return carry
-
-    lax.fori_loop(0, 16, some, 0)
+    for j in range(16):
+        await_bytes(arrived.at[pl.ds(40 * j, 40)], recv_sem.at[j])
+        for i in range(8 * j, 8 * j + 8):
+            for q in range(5):
+                rows = arrived[5 * i + q].astype(F32)
+                at = i * BLOCK + 4 * q
+                y[at : at + 4, :] = rows
+                y[DEV * BLOCK + at : DEV * BLOCK + at + 4, :] = pltpu.roll(rows, 64, 1)
 
 
 def block(k):
@@ -229,37 +226,29 @@
 def share(phase, buf, send_sem, recv_sem, wait=False):
     members, me, target = group(phase)
     leaf, (x, z, y, core) = lax.axis_index("leaf"), place()
-
-    def copy_to(i, c, to):
-        return pltpu.make_async_remote_copy(
-            src_ref=buf.at[me],
-            dst_ref=buf.at[me],
-            send_sem=send_sem.at[phase, 2 * i + c],
-            recv_sem=recv_sem.at[phase, me],
-            device_id=to,
-            device_id_type=MESH,
-        )
-
-    def act(copy):
-        if wait:
-            copy.wait_send()
+    others = buf.at[pl.ds(0, members - 1)]
+
+    def copy_to(c, to):
+        return remote(buf.at[me], buf.at[me], send_sem.at[phase, c], recv_sem.at[phase], to)
+
+    if phase == 0:
+        if not wait:
+            copy_to(0, {"leaf": leaf, "sub": y * 2 + 1 - core}).start()
         else:
-            copy.start()
-
-    if phase == 0:
-        act(copy_to(1, 0, {"leaf": leaf, "sub": y * 2 + 1 - core}))
+            await_bytes(others, send_sem.at[phase, 0])
     else:
 
         @pl.when(core == 1)
         def _():
-            for i in (2, 1, 3):
-                for c in range(2):
-                    act(copy_to(i, c, target(lax.rem(me + i, members), c)))
+            for c in range(2):
+                if wait:
+                    await_bytes(others, send_sem.at[phase, c])
+                    continue
+                for i in (2, 1, 3):
+                    copy_to(c, target(lax.rem(me + i, members), c)).start()
 
     if wait:
-        for i in range(1, members):
-            other = lax.rem(me + i, members)
-            pltpu.make_async_copy(buf.at[other], buf.at[other], recv_sem.at[phase, other]).wait()
+        await_bytes(others, recv_sem.at[phase])
 
 
 def fold(a):
@@ -272,12 +261,14 @@
 
 def kernel(
     counts,
+    codes_h,
     slots_h,
     vec_h,
     inverse_h,
     left_h,
     right_h,
     out_h,
+    codes,
     slots_ref,
     vec,
     out,
@@ -291,6 +282,8 @@
     flat,
     x,
     stage,
+    pos_src,
+    pos_dst,
     src1,
     dst1,
     src2,
@@ -311,6 +304,7 @@
     g_d,
     partner,
     load_sem,
+    pos_sem,
     index_sem,
     send_sem,
     recv1,
@@ -326,6 +320,7 @@
             pltpu.make_async_copy(h, v, load_sem.at[i])
             for i, (h, v) in enumerate(
                 (
+                    (codes_h, codes),
                     (slots_h, slots_ref),
                     (vec_h, vec),
                     (left_h, left),
@@ -339,34 +334,41 @@
         enter()
     with jax.named_scope("route"):
         loads[0].wait()
-        live, owner, ranks, base, total = route(counts, slots_ref, rank_ref)
-        flat_v[...] = jnp.clip(jnp.where(live, bucket_row(owner, ranks), 0), 0, 2 * DEV * BLOCK - 1)
+        loads[1].wait()
+        live, owner, ranks, base, total = route(counts, slots_ref, codes, rank_ref)
+        rows = jnp.where(live, bucket_row(owner, ranks), 0).astype(F32)
+        rows = jnp.concatenate([rows, jnp.zeros((DEV - 40, 128), F32)], axis=0).T.astype(I32)
+        flat_v[...] = jnp.clip(rows, 0, 2 * DEV * BLOCK - 1)
         both = total[:, :128].astype(I32)
         source = both * 128 + pltpu.roll(both, 64, 1)
         lane128 = iota((DEV, 128), 1)
-        pick_v[...] = jnp.clip(jnp.where(lane128 < PEER, source, 0), 0, SLOTS - 1)
+        pick_v[...] = jnp.clip(source.astype(F32).T[:PEER].astype(I32), 0, SLOTS - 1)
         pick_copy = pltpu.make_async_copy(pick_v, pick, index_sem.at[0])
         pick_copy.start()
         flat_copy = pltpu.make_async_copy(flat_v, flat, index_sem.at[1])
         flat_copy.start()
         position = total[:, 128:]
-        x[SLOTS : SLOTS + DEV, :] = jnp.where(lane128.astype(F32) < base, position, 64.0)
-        x[SLOTS + DEV :, :] = pltpu.roll(position, 64, 1)
+        spot = position * 64.0 + pltpu.roll(position, 64, 1)
+        pos_src[...] = jnp.where(lane128.astype(F32) < base, spot, float(ROWS)).reshape(DEV, 1, 128)
+        pos_dst[DEV - 1] = pos_src[DEV - 1]
     with jax.named_scope("rows"):
-        loads[1].wait()
+        loads[2].wait()
         for a in range(40):
             part = vec[:, a * 128 : (a + 1) * 128].astype(F32)
             x[a * 128 : (a + 1) * 128, :] = jnp.concatenate([part, part], axis=0).T
-        for u in range(8):
-            stage[u] = jnp.zeros((BLOCK, 128), F32)
         pick_copy.wait()
     with jax.named_scope("entered"):
         entered()
+    with jax.named_scope("positions"):
+        for c in range(16):
+            for u, to in enumerate(group_of(c, 1)[: 8 if c < 15 else 7]):
+                i = 16 * u + c
+                remote(pos_src.at[i], pos_dst.at[i], pos_sem.at[0], pos_sem.at[1], to).start()
     with jax.named_scope("send"):
-        gather_and_send(pick, x, stage, src1, dst1, send_sem.at[0], recv1)
+        gather_and_send(pick, x, stage, src1, dst1, send_sem.at[0], recv1, 1)
     with jax.named_scope("gram"):
-        loads[2].wait()
         loads[3].wait()
+        loads[4].wait()
         gram = jnp.zeros((CROSS * RANK - RANK, CROSS * RANK), F32)
         for c in range(4):
             at = slice(c * 1024, (c + 1) * 1024)
@@ -382,23 +384,15 @@
                     j * RANK : (j + 1) * RANK, k * RANK : (k + 1) * RANK
                 ].astype(BF16)
         share(0, g_a, send_g, recv_g)
-    with jax.named_scope("gram_y"):
-        share(0, g_a, send_g, recv_g, wait=True)
-        ysum = g_a[0].astype(F32) + g_a[1].astype(F32)
-        mine = group(1)[1]
-        g_b[mine, :160] = ysum[:160, :128].astype(BF16)
-        g_b[mine, 160:] = ysum[128:160, 128:].astype(BF16)
-    with jax.named_scope("receive"):
-        receive(dst1, recv1, y)
     with jax.named_scope("inv"):
-        high = y[pl.ds(20, DEV, stride=BLOCK), :]
-        low = y[pl.ds(21, DEV, stride=BLOCK), :]
-        spot = high.astype(I32) * 64 + low.astype(I32)
-        back_v[...] = jnp.clip(jnp.where(lane128 < PEER, spot, 0), 0, ROWS - 1)
+        await_bytes(pos_dst.at[pl.ds(0, DEV - 1)], pos_sem.at[1])
+        await_bytes(pos_src.at[pl.ds(0, DEV - 1)], pos_sem.at[0])
+        spot = pos_dst[...].reshape(DEV, 128).astype(I32)
+        back_v[...] = jnp.clip(spot.astype(F32).T[:PEER].astype(I32), 0, ROWS - 1)
         back_copy = pltpu.make_async_copy(back_v, back, index_sem.at[2])
         back_copy.start()
-        high_t = high.T
-        low_t = low.T
+        high_t = (spot >> 6).astype(F32).T
+        low_t = (spot & 63).astype(F32).T
         ids = iota((64, 128), 0).astype(F32)
         lanes = iota((64, 128), 1).astype(F32)
         found = jnp.zeros((64, 128), F32)
@@ -417,18 +411,27 @@
         )
         inv_copy = pltpu.make_async_copy(inv_v, inv, index_sem.at[3])
         inv_copy.start()
+    with jax.named_scope("gram_y"):
+        share(0, g_a, send_g, recv_g, wait=True)
+        ysum = g_a[0].astype(F32) + g_a[1].astype(F32)
+        mine = group(1)[1]
+        g_b[mine, :160] = ysum[:160, :128].astype(BF16)
+        g_b[mine, 160:] = ysum[128:160, 128:].astype(BF16)
+    with jax.named_scope("receive"):
+        receive(dst1, recv1, y)
         share(1, g_b, send_g, recv_g)
         inv_copy.wait()
     with jax.named_scope("tree"):
-
-        def some(c, carry):
+        loads[5].wait()
+
+        def pull(c, carry):
             for u in range(128):
-                x[pl.ds(c * 128 + u, 1), :] = y[pl.ds(inv[c * 2 + u // 64, u % 64], 1), :]
+                at = pl.ds(u * 32 + c, 1)
+                x[at, :] = y[pl.ds(inv.at[u // 2, pl.ds(u % 2 * 32, 32)][c], 1), :]
             return carry
 
-        lax.fori_loop(0, ROWS // 128, some, 0)
+        lax.fori_loop(0, 32, pull, 0)
     with jax.named_scope("leaf"):
-        loads[4].wait()
         for l in range(ROWS // LEAF):
             at = slice(l * LEAF, (l + 1) * LEAF)
             field[:, at] = dot_nt(x[at, :].T[:VECS].astype(BF16), inverse[l])
@@ -540,31 +543,32 @@
         back_copy.wait()
         sent(src1, send_sem.at[0])
     with jax.named_scope("send_back"):
-        gather_and_send(back, x, stage, src2, dst2, send_sem.at[1], recv2)
+        gather_and_send(back, x, stage, src2, dst2, send_sem.at[1], recv2, -1)
     with jax.named_scope("receive_back"):
         flat_copy.wait()
         receive(dst2, recv2, y)
     with jax.named_scope("output"):
         alive = jnp.where(live_slots(counts, slots_ref[...]), 1, 0)
 
-        def pull(c):
+        slots_ref[...] = alive
+
+        def pull_slots(a):
             for u in range(128):
-                x[pl.ds(pl.multiple_of(c * 128, 128) + u, 1), :] = y[pl.ds(flat[c, u], 1), :]
+                x[pl.ds(pl.multiple_of(a * 128, 128) + u, 1), :] = y[pl.ds(flat.at[u][a], 1), :]
 
         def push(a):
             at = pl.multiple_of(a * 128, 128)
             part = x[pl.ds(at, 128), :].T[:VECS]
             out[:, pl.ds(at, 128)] = jnp.where(slots_ref[pl.ds(a, 1), :] > 0, part, 0.0).astype(BF16)
 
-        slots_ref[...] = alive
-        pull(0)
-
-        def step(c, carry):
-            pull(c + 1)
-            push(c)
+        pull_slots(0)
+
+        def next_slots(a, carry):
+            push(a)
+            pull_slots(a + 1)
             return carry
 
-        lax.fori_loop(0, 39, step, 0)
+        lax.fori_loop(0, 39, next_slots, 0)
         push(39)
         store = pltpu.make_async_copy(out, out_h, load_sem.at[0])
         store.start()
@@ -575,26 +579,29 @@
 def body(vectors, row_counts, tree_slot, leaf_inverse, left_basis, right_basis):
     anywhere = pl.BlockSpec(memory_space=pl.ANY)
     dma = pltpu.SemaphoreType.DMA
-    blocks = pltpu.VMEM((DEV, BLOCK, 128), BF16)
+    blocks = pltpu.VMEM((DEV * 5, 4, 128), BF16)
     return pl.pallas_call(
         kernel,
         out_shape=jax.ShapeDtypeStruct((VECS, SLOTS), BF16),
-        in_specs=[SMEM] + [anywhere] * 5,
+        in_specs=[SMEM] + [anywhere] * 6,
         out_specs=anywhere,
         scratch_shapes=[
+            pltpu.VMEM((DEV, 128), I32),
             pltpu.VMEM((40, 128), I32),
             pltpu.VMEM((VECS, SLOTS), BF16),
             pltpu.VMEM((VECS, SLOTS), BF16),
             pltpu.VMEM(leaf_inverse.shape, BF16),
             pltpu.VMEM(left_basis.shape, BF16),
             pltpu.VMEM(right_basis.shape, BF16),
+            pltpu.VMEM((PEER, DEV), I32),
+            pltpu.SMEM((PEER, DEV), I32),
+            pltpu.VMEM((40, 128), F32),
             pltpu.VMEM((DEV, 128), I32),
             pltpu.SMEM((DEV, 128), I32),
-            pltpu.VMEM((40, 128), F32),
-            pltpu.VMEM((40, 128), I32),
-            pltpu.SMEM((40, 128), I32),
-            pltpu.VMEM((SLOTS + 2 * DEV, 128), F32),
+            pltpu.VMEM((SLOTS, 128), F32),
             pltpu.VMEM((8, BLOCK, 128), F32),
+            pltpu.VMEM((DEV, 1, 128), F32),
+            pltpu.VMEM((DEV, 1, 128), F32),
             blocks,
             blocks,
             blocks,
@@ -602,8 +609,8 @@
             pltpu.VMEM((2 * DEV * BLOCK, 128), F32),
             pltpu.VMEM((64, 128), I32),
             pltpu.SMEM((64, 128), I32),
-            pltpu.VMEM((DEV, 128), I32),
-            pltpu.SMEM((DEV, 128), I32),
+            pltpu.VMEM((PEER, DEV), I32),
+            pltpu.SMEM((PEER, DEV), I32),
             pltpu.VMEM((VECS, ROWS), F32),
             pltpu.VMEM((2, VECS, 256), F32),
             pltpu.VMEM((4, 96, 128), BF16),
@@ -614,19 +621,23 @@
             pltpu.VMEM((4, 96, 128), BF16),
             pltpu.VMEM((4, 32, 128), BF16),
             pltpu.VMEM((VECS, 256), BF16),
-            dma((5,)),
+            dma((6,)),
+            dma((2,)),
             dma((4,)),
             dma((2,)),
-            dma((DEV,)),
-            dma((DEV,)),
-            dma((4, 8)),
-            dma((4, 4)),
-            dma((4, 8)),
-            dma((4, 4)),
+            dma((16,)),
+            dma((16,)),
+            dma((4, 2)),
+            dma((4,)),
+            dma((4, 2)),
+            dma((4,)),
         ],
         compiler_params=pltpu.CompilerParams(collective_id=0, has_side_effects=True),
         name="apply",
-    )(row_counts, tree_slot.reshape(40, 128), vectors, leaf_inverse, left_basis, right_basis)
+    )(
+        row_counts,
+        jnp.asarray(np.repeat(CODES[:, None], 128, 1)),
+        tree_slot.reshape(40, 128), vectors, leaf_inverse, left_basis, right_basis)
 
 
 def solution(mesh):

time: 74.6 us -> 65.4 us (0.88)
  Pallas kernels: 72.5 us -> 63.2 us
    pallas_call x1, Pallas kernels: 72.5 us -> 63.2 us  [body(): pl.pallas_call(kernel, out_shape=jax.ShapeDtypeStruct((VECS, SLOTS), BF16...]
where the time goes in v2:
time: 65.4 us; the launch traced here: 65.2 us
  Pallas kernels  63.2 us (97%)
  local copies, waits for them, and re-layouts  1.97 us (3%)
    pallas_call x1, Pallas kernels, body(): pl.pallas_call(kernel, out_shape=jax.ShapeDtypeStruct((VECS, SLOTS), BF16...  63.2 us
    unnamed x1, local copies, waits for them, and re-layouts  1.97 us

profile of v2, /device:TPU:1, one launch (start us, length us, event | category | flops | bytes accessed | tf_op | source)
XLA Modules:
  0.0 65.2 jit_solution(12132245520533076579)
XLA Ops:
  0.0 63.2 %apply.1 = bf16[64,5120]{1,0:T(8,128)(2,1)} custom-call(s32[128]{0:T(128)} %counts.1, s32[128,128]{1,0:T(8,128)} %constant.2.clone.codes_h, s32[40,128]{1,0:T(8,128)} %bitcast.1, bf16[64,5120]{1,0:T(8,128)(2,1)} %vec_h.1, bf16[16,256,256]{2,1,0:T(8,128)(2,1)} %inverse_h.1, bf16[11,32,4096]{2,1,0:T(8,128)(2,1)} %left_h.1, bf16[11,32,4096]{2,1,0:T(8,128)(2,1)} %right_h.1), custom_call_target="tpu_custom_call" | custom-call | tf_op jit(solution)/shard_map/apply/pallas_call | solution.py:583
  63.2 2.0 %copy.9 = bf16[64,5120]{1,0:T(8,128)(2,1)} copy(bf16[64,5120]{1,0:T(8,128)(2,1)} %apply.1) | data formatting | bytes 1310720

commit v3 on v2

--- a/solution.py
+++ b/solution.py
@@ -20,6 +20,7 @@
 RANK = 32
 LOCAL = 4
 CROSS = 7
+LEVELS = 11
 F32 = jnp.float32
 BF16 = jnp.bfloat16
 I32 = jnp.int32
@@ -111,7 +112,7 @@
     r64 = iota((64, 128), 0)
     lane = iota((64, 128), 1).astype(F32)
     total = jnp.zeros((DEV, 256), F32)
-    for a in range(40):
+    def tables(a):
         hit = jnp.where(ids == owner[a : a + 1, :], 1.0, 0.0).astype(BF16)
         match = r64 == ranks[a : a + 1, :]
         table = jnp.concatenate(
@@ -123,7 +124,11 @@
             ],
             axis=0,
         ).astype(BF16)
-        total = total + dot_nt(hit, table)
+        return hit, table
+
+    for a in range(0, 40, 2):
+        hits, parts = zip(tables(a), tables(a + 1))
+        total = total + dot_nt(jnp.concatenate(hits, axis=1), jnp.concatenate(parts, axis=1))
     return live, found >> 6, ranks, base - start, total
 
 
@@ -184,8 +189,8 @@
     send(15)
 
 
-def receive(arrived, recv_sem, y):
-    for j in range(16):
+def receive(arrived, recv_sem, y, groups=range(16)):
+    for j in groups:
         await_bytes(arrived.at[pl.ds(40 * j, 40)], recv_sem.at[j])
         for i in range(8 * j, 8 * j + 8):
             for q in range(5):
@@ -303,6 +308,8 @@
     g_c,
     g_d,
     partner,
+    g_l,
+    near,
     load_sem,
     pos_sem,
     index_sem,
@@ -324,17 +331,20 @@
                     (slots_h, slots_ref),
                     (vec_h, vec),
                     (left_h, left),
-                    (right_h, right),
                     (inverse_h, inverse),
                 )
             )
         ]
-        for load in loads:
+        for load in loads[:3]:
             load.start()
         enter()
     with jax.named_scope("route"):
         loads[0].wait()
         loads[1].wait()
+        for load in loads[3:]:
+            load.start()
+        for k in range(LEVELS):
+            pltpu.make_async_copy(right_h.at[k], right.at[LEVELS - 1 - k], load_sem.at[5]).start()
         live, owner, ranks, base, total = route(counts, slots_ref, codes, rank_ref)
         rows = jnp.where(live, bucket_row(owner, ranks), 0).astype(F32)
         rows = jnp.concatenate([rows, jnp.zeros((DEV - 40, 128), F32)], axis=0).T.astype(I32)
@@ -368,21 +378,26 @@
         gather_and_send(pick, x, stage, src1, dst1, send_sem.at[0], recv1, 1)
     with jax.named_scope("gram"):
         loads[3].wait()
-        loads[4].wait()
-        gram = jnp.zeros((CROSS * RANK - RANK, CROSS * RANK), F32)
-        for c in range(4):
-            at = slice(c * 1024, (c + 1) * 1024)
-            gram = gram + dot_nt(
-                left[LOCAL : LOCAL + 6, :, at].reshape(6 * RANK, 1024),
-                right[LOCAL:, :, at].reshape(CROSS * RANK, 1024),
+        await_bytes(right, load_sem.at[5])
+        sums = [None] * LOCAL
+        cross = None
+        for b in range(16):
+            at = slice(b * LEAF, (b + 1) * LEAF)
+            gram = dot_nt(
+                left[: LEVELS - 1, :, at].reshape(10 * RANK, LEAF),
+                right[: LEVELS - 1, :, at].reshape(10 * RANK, LEAF),
             )
+            for j in range(LOCAL):
+                part = gram[j * RANK : (j + 1) * RANK]
+                sums[j] = part if b % 2**j == 0 else sums[j] + part
+                if (b + 1) % 2**j == 0:
+                    g_l[32 - 2 ** (5 - j) + b // 2**j, :, : 10 * RANK] = sums[j].astype(BF16)
+            part = gram[LOCAL * RANK :, : CROSS * RANK]
+            cross = part if b == 0 else cross + part
         core = group(0)[1]
         g_a[core] = jnp.zeros((192, 256), BF16)
         for j in range(CROSS - 1):
-            for k in range(j + 1, CROSS):
-                g_a[core, rows_of(j), block(k)] = gram[
-                    j * RANK : (j + 1) * RANK, k * RANK : (k + 1) * RANK
-                ].astype(BF16)
+            g_a[core, rows_of(j), : CROSS * RANK] = cross[j * RANK : (j + 1) * RANK].astype(BF16)
         share(0, g_a, send_g, recv_g)
     with jax.named_scope("inv"):
         await_bytes(pos_dst.at[pl.ds(0, DEV - 1)], pos_sem.at[1])
@@ -396,13 +411,16 @@
         ids = iota((64, 128), 0).astype(F32)
         lanes = iota((64, 128), 1).astype(F32)
         found = jnp.zeros((64, 128), F32)
-        for r in range(PEER):
+
+        def tables(r):
             hit = jnp.where(ids == high_t[r : r + 1, :], 1.0, 0.0).astype(BF16)
             match = ids == low_t[r : r + 1, :]
-            table = jnp.concatenate(
-                [jnp.where(match, lanes, 0.0), jnp.where(match, float(r), 0.0)], axis=0
-            ).astype(BF16)
-            found = found + dot_nt(hit, table)
+            table = [jnp.where(match, lanes, 0.0), jnp.where(match, float(r), 0.0)]
+            return hit, jnp.concatenate(table, axis=0).astype(BF16)
+
+        for r in range(0, PEER, 2):
+            hits, parts = zip(tables(r), tables(r + 1))
+            found = found + dot_nt(jnp.concatenate(hits, axis=1), jnp.concatenate(parts, axis=1))
         whole = found.astype(I32)
         inv_v[...] = jnp.clip(
             jnp.where(iota((64, 128), 1) < 64, bucket_row(whole, pltpu.roll(whole, 64, 1)), 0),
@@ -418,11 +436,11 @@
         g_b[mine, :160] = ysum[:160, :128].astype(BF16)
         g_b[mine, 160:] = ysum[128:160, 128:].astype(BF16)
     with jax.named_scope("receive"):
-        receive(dst1, recv1, y)
+        receive(dst1, recv1, y, range(12))
         share(1, g_b, send_g, recv_g)
+        receive(dst1, recv1, y, range(12, 16))
         inv_copy.wait()
     with jax.named_scope("tree"):
-        loads[5].wait()
 
         def pull(c, carry):
             for u in range(128):
@@ -432,6 +450,7 @@
 
         lax.fori_loop(0, 32, pull, 0)
     with jax.named_scope("leaf"):
+        loads[4].wait()
         for l in range(ROWS // LEAF):
             at = slice(l * LEAF, (l + 1) * LEAF)
             field[:, at] = dot_nt(x[at, :].T[:VECS].astype(BF16), inverse[l])
@@ -443,36 +462,29 @@
         g_c[group(2)[1]] = zsum.astype(BF16)
         share(2, g_c, send_g, recv_g)
     with jax.named_scope("local"):
-        for level in range(LOCAL):
-            size = LEAF * 2**level
-            nodes = ROWS // size
-
-            def pair(m, carry):
-                at = [pl.multiple_of(m * 2 * size, size), pl.multiple_of(m * 2 * size + size, size)]
-                coeff = [
-                    (
-                        dot_nt(field[:, pl.ds(s, size)].astype(BF16), right[level, :, pl.ds(s, size)])
-                        * (1.0 / math.sqrt(size))
-                    ).astype(BF16)
-                    for s in at
+        vs = [
+            dot_nt(
+                field[:, b * LEAF : (b + 1) * LEAF].astype(BF16),
+                right[:, :, b * LEAF : (b + 1) * LEAF].reshape(LEVELS * RANK, LEAF),
+            )
+            for b in range(16)
+        ]
+        for k in range(LOCAL):
+            rest = (LEVELS - 1 - k) * RANK
+            merged = []
+            for m in range(len(vs) // 2):
+                va, vb = vs[2 * m], vs[2 * m + 1]
+                p2 = [
+                    (v[:, rest : rest + RANK] * (1.0 / math.sqrt(LEAF * 2**k))).astype(BF16) for v in (vb, va)
                 ]
+                first = 32 - 2 ** (5 - k) + 2 * m
+                g2 = jnp.concatenate([g_l[first, :, :rest], g_l[first + 1, :, :rest]], axis=0)
+                merged.append(va[:, :rest] + vb[:, :rest] - dot(jnp.concatenate(p2, axis=1), g2))
                 for n in range(2):
-                    field[:, pl.ds(at[n], size)] -= dot(coeff[1 - n], left[level, :, pl.ds(at[n], size)])
-                return carry
-
-            lax.fori_loop(0, nodes // 2, pair, 0, unroll=True)
-    with jax.named_scope("gram_x"):
-        share(2, g_c, send_g, recv_g, wait=True)
-        xsum = (g_c[0, :32].astype(F32) + g_c[1, :32].astype(F32)) + (
-            g_c[2, :32].astype(F32) + g_c[3, :32].astype(F32)
-        )
-        g_d[group(3)[1]] = xsum.astype(BF16)
-        share(3, g_d, send_g, recv_g)
-    with jax.named_scope("reduce"):
-        v = jnp.zeros((VECS, CROSS * RANK), F32)
-        for c in range(4):
-            at = slice(c * 1024, (c + 1) * 1024)
-            v = v + dot_nt(field[:, at].astype(BF16), right[LOCAL:, :, at].reshape(CROSS * RANK, 1024))
+                    for b in range((2 * m + n) * 2**k, (2 * m + n + 1) * 2**k):
+                        near[b, :, k * RANK : (k + 1) * RANK] = p2[n]
+            vs = merged
+        v = vs[0]
 
     def level_rows(k, g):
         if k == 1:
@@ -493,9 +505,8 @@
 
     with jax.named_scope("cross_core"):
         core = group(0)[1]
-        v_a[core] = jnp.zeros((VECS, 256), F32)
-        for k in range(CROSS):
-            v_a[core, :, block(k)] = v[:, k * RANK : (k + 1) * RANK]
+        v_a[core, :, 192:] = jnp.zeros((VECS, 64), F32)
+        v_a[core, :, : CROSS * RANK] = v
         share(0, v_a, send_v, recv_v)
         share(0, v_a, send_v, recv_v, wait=True)
         pa, pb, v = merge(0, v_a[0], v_a[1], g_a[0], g_a[1])
@@ -512,6 +523,16 @@
         else:
             v_buf[me] = fold(v).astype(BF16)
         share(phase, v_buf, send_v, recv_v)
+        if phase == 1:
+            share(2, g_c, send_g, recv_g, wait=True)
+            xsum = (g_c[0, :32].astype(F32) + g_c[1, :32].astype(F32)) + (
+                g_c[2, :32].astype(F32) + g_c[3, :32].astype(F32)
+            )
+            g_d[group(3)[1]] = xsum.astype(BF16)
+            share(3, g_d, send_g, recv_g)
+            for b in range(16):
+                at = slice(b * LEAF, (b + 1) * LEAF)
+                field[:, at] -= dot(near[b], left[:LOCAL, :, at].reshape(LOCAL * RANK, LEAF))
         share(phase, v_buf, send_v, recv_v, wait=True)
         vs = [v_buf[i].astype(F32) for i in range(4)]
         if phase == 1:
@@ -562,17 +583,27 @@
             out[:, pl.ds(at, 128)] = jnp.where(slots_ref[pl.ds(a, 1), :] > 0, part, 0.0).astype(BF16)
 
         pull_slots(0)
-
-        def next_slots(a, carry):
-            push(a)
-            pull_slots(a + 1)
+        pull_slots(1)
+
+        def next_slots(c, carry):
+            push(2 * c)
+            push(2 * c + 1)
+            pull_slots(2 * c + 2)
+            pull_slots(2 * c + 3)
             return carry
 
-        lax.fori_loop(0, 39, next_slots, 0)
-        push(39)
-        store = pltpu.make_async_copy(out, out_h, load_sem.at[0])
-        store.start()
-        store.wait()
+        stores = []
+        for part in range(4):
+            lax.fori_loop(5 * part, 5 * part + 5 - part // 3, next_slots, 0)
+            if part == 3:
+                push(38)
+                push(39)
+            at = pl.ds(part * 1280, 1280)
+            store = pltpu.make_async_copy(out.at[:, at], out_h.at[:, at], load_sem.at[part])
+            store.start()
+            stores.append(store)
+        for store in stores:
+            store.wait()
         sent(src2, send_sem.at[1])
 
 
@@ -621,6 +652,8 @@
             pltpu.VMEM((4, 96, 128), BF16),
             pltpu.VMEM((4, 32, 128), BF16),
             pltpu.VMEM((VECS, 256), BF16),
+            pltpu.VMEM((30, RANK, 384), BF16),
+            pltpu.VMEM((16, VECS, LOCAL * RANK), BF16),
             dma((6,)),
             dma((2,)),
             dma((4,)),

time: 65.4 us -> 60.6 us (0.927)
  Pallas kernels: 63.2 us -> 58.5 us
    pallas_call x1, Pallas kernels: 63.2 us -> 58.5 us  [body(): pl.pallas_call(kernel, out_shape=jax.ShapeDtypeStruct((VECS, SLOTS), BF16...]
where the time goes in v3:
time: 60.6 us; the launch traced here: 60.5 us
  Pallas kernels  58.5 us (97%)
  local copies, waits for them, and re-layouts  1.97 us (3%)
    pallas_call x1, Pallas kernels, body(): pl.pallas_call(kernel, out_shape=jax.ShapeDtypeStruct((VECS, SLOTS), BF16...  58.5 us
    unnamed x1, local copies, waits for them, and re-layouts  1.97 us

profile of v3, /device:TPU:1, one launch (start us, length us, event | category | flops | bytes accessed | tf_op | source)
XLA Modules:
  0.0 60.5 jit_solution(6373926654823436743)
XLA Ops:
  0.0 58.5 %apply.1 = bf16[64,5120]{1,0:T(8,128)(2,1)} custom-call(s32[128]{0:T(128)} %counts.1, s32[128,128]{1,0:T(8,128)} %constant.2.clone.codes_h, s32[40,128]{1,0:T(8,128)} %bitcast.1, bf16[64,5120]{1,0:T(8,128)(2,1)} %vec_h.1, bf16[16,256,256]{2,1,0:T(8,128)(2,1)} %inverse_h.1, bf16[11,32,4096]{2,1,0:T(8,128)(2,1)} %left_h.1, bf16[11,32,4096]{2,1,0:T(8,128)(2,1)} %right_h.1), custom_call_target="tpu_custom_call" | custom-call | tf_op jit(solution)/shard_map/apply/pallas_call | solution.py:614
  58.5 2.0 %copy.9 = bf16[64,5120]{1,0:T(8,128)(2,1)} copy(bf16[64,5120]{1,0:T(8,128)(2,1)} %apply.1) | data formatting | bytes 1310720

commit v4 on v3

--- a/solution.py
+++ b/solution.py
@@ -221,39 +221,23 @@
     x, z, y, core = place()
     leaf, sub = lax.axis_index("leaf"), lax.axis_index("sub")
     return [
-        (2, core, None),
-        (4, y, lambda m, c: {"leaf": leaf, "sub": m * 2 + c}),
-        (4, z, lambda m, c: {"leaf": x * 4 + m, "sub": y * 2 + c}),
-        (4, x, lambda m, c: {"leaf": m * 4 + z, "sub": y * 2 + c}),
+        (2, core, lambda m: {"leaf": leaf, "sub": y * 2 + m}),
+        (4, y, lambda m: {"leaf": leaf, "sub": m * 2 + core}),
+        (4, z, lambda m: {"leaf": x * 4 + m, "sub": sub}),
+        (4, x, lambda m: {"leaf": m * 4 + z, "sub": sub}),
     ][phase]
 
 
 def share(phase, buf, send_sem, recv_sem, wait=False):
     members, me, target = group(phase)
-    leaf, (x, z, y, core) = lax.axis_index("leaf"), place()
     others = buf.at[pl.ds(0, members - 1)]
-
-    def copy_to(c, to):
-        return remote(buf.at[me], buf.at[me], send_sem.at[phase, c], recv_sem.at[phase], to)
-
-    if phase == 0:
-        if not wait:
-            copy_to(0, {"leaf": leaf, "sub": y * 2 + 1 - core}).start()
-        else:
-            await_bytes(others, send_sem.at[phase, 0])
-    else:
-
-        @pl.when(core == 1)
-        def _():
-            for c in range(2):
-                if wait:
-                    await_bytes(others, send_sem.at[phase, c])
-                    continue
-                for i in (2, 1, 3):
-                    copy_to(c, target(lax.rem(me + i, members), c)).start()
-
     if wait:
+        await_bytes(others, send_sem.at[phase])
         await_bytes(others, recv_sem.at[phase])
+        return
+    for i in (1,) if members == 2 else (2, 1, 3):
+        to = target(lax.rem(me + i, members))
+        remote(buf.at[me], buf.at[me], send_sem.at[phase], recv_sem.at[phase], to).start()
 
 
 def fold(a):
@@ -312,6 +296,7 @@
     near,
     load_sem,
     pos_sem,
+    part_sem,
     index_sem,
     send_sem,
     recv1,
@@ -431,13 +416,21 @@
         inv_copy.start()
     with jax.named_scope("gram_y"):
         share(0, g_a, send_g, recv_g, wait=True)
-        ysum = g_a[0].astype(F32) + g_a[1].astype(F32)
-        mine = group(1)[1]
-        g_b[mine, :160] = ysum[:160, :128].astype(BF16)
-        g_b[mine, 160:] = ysum[128:160, 128:].astype(BF16)
+
+        @pl.when(core == 1)
+        def _():
+            ysum = g_a[0].astype(F32) + g_a[1].astype(F32)
+            mine = group(1)[1]
+            g_b[mine, :160] = ysum[:160, :128].astype(BF16)
+            g_b[mine, 160:] = ysum[128:160, 128:].astype(BF16)
+
     with jax.named_scope("receive"):
         receive(dst1, recv1, y, range(12))
-        share(1, g_b, send_g, recv_g)
+
+        @pl.when(core == 1)
+        def _():
+            share(1, g_b, send_g, recv_g)
+
         receive(dst1, recv1, y, range(12, 16))
         inv_copy.wait()
     with jax.named_scope("tree"):
@@ -455,12 +448,16 @@
             at = slice(l * LEAF, (l + 1) * LEAF)
             field[:, at] = dot_nt(x[at, :].T[:VECS].astype(BF16), inverse[l])
     with jax.named_scope("gram_z"):
-        share(1, g_b, send_g, recv_g, wait=True)
-        zsum = (g_b[0, :96, :128].astype(F32) + g_b[1, :96, :128].astype(F32)) + (
-            g_b[2, :96, :128].astype(F32) + g_b[3, :96, :128].astype(F32)
-        )
-        g_c[group(2)[1]] = zsum.astype(BF16)
-        share(2, g_c, send_g, recv_g)
+
+        @pl.when(core == 1)
+        def _():
+            share(1, g_b, send_g, recv_g, wait=True)
+            zsum = (g_b[0, :96, :128].astype(F32) + g_b[1, :96, :128].astype(F32)) + (
+                g_b[2, :96, :128].astype(F32) + g_b[3, :96, :128].astype(F32)
+            )
+            g_c[group(2)[1]] = zsum.astype(BF16)
+            share(2, g_c, send_g, recv_g)
+
     with jax.named_scope("local"):
         vs = [
             dot_nt(
@@ -500,21 +497,23 @@
         g2 = jnp.concatenate([level_rows(k, ga), level_rows(k, gb)], axis=0).astype(BF16)
         return pa, pb, va[:, above(k)] + vb[:, above(k)] - dot(p2, g2)
 
-    def keep(k, p):
-        partner[:, k * RANK : (k + 1) * RANK] = p
-
     with jax.named_scope("cross_core"):
-        core = group(0)[1]
+        partner[:, 6 * RANK :] = jnp.zeros((VECS, 256 - 6 * RANK), BF16)
         v_a[core, :, 192:] = jnp.zeros((VECS, 64), F32)
         v_a[core, :, : CROSS * RANK] = v
         share(0, v_a, send_v, recv_v)
         share(0, v_a, send_v, recv_v, wait=True)
-        pa, pb, v = merge(0, v_a[0], v_a[1], g_a[0], g_a[1])
-        keep(0, jnp.where(core == 0, pa, pb))
-
-    def four(phase, k, v, v_buf, g_buf):
+        mine = (v_a[1 - core, :, block(0)] * scale[0]).astype(BF16)
+
+    def near_update():
+        for b in range(16):
+            at = slice(b * LEAF, (b + 1) * LEAF)
+            field[:, at] -= dot(near[b], left[:LOCAL, :, at].reshape(LOCAL * RANK, LEAF)) + dot(
+                mine, left[LOCAL, :, at]
+            )
+
+    def four(phase, k, v, v_buf, g_buf, meanwhile):
         me = group(phase)[1]
-        v = v.astype(BF16).astype(F32)
         if phase == 1:
             v_buf[me, :64] = v[:, :128].astype(BF16)
             v_buf[me, 64:] = fold(v[:, 128:]).astype(BF16)
@@ -523,16 +522,7 @@
         else:
             v_buf[me] = fold(v).astype(BF16)
         share(phase, v_buf, send_v, recv_v)
-        if phase == 1:
-            share(2, g_c, send_g, recv_g, wait=True)
-            xsum = (g_c[0, :32].astype(F32) + g_c[1, :32].astype(F32)) + (
-                g_c[2, :32].astype(F32) + g_c[3, :32].astype(F32)
-            )
-            g_d[group(3)[1]] = xsum.astype(BF16)
-            share(3, g_d, send_g, recv_g)
-            for b in range(16):
-                at = slice(b * LEAF, (b + 1) * LEAF)
-                field[:, at] -= dot(near[b], left[:LOCAL, :, at].reshape(LOCAL * RANK, LEAF))
+        meanwhile()
         share(phase, v_buf, send_v, recv_v, wait=True)
         vs = [v_buf[i].astype(F32) for i in range(4)]
         if phase == 1:
@@ -542,23 +532,58 @@
         gs = [g_buf[i].astype(F32) for i in range(4)]
         p0, p1, v01 = merge(k, vs[0], vs[1], gs[0], gs[1])
         p2, p3, v23 = merge(k, vs[2], vs[3], gs[2], gs[3])
-        keep(k, jnp.where(me < 2, jnp.where(me == 0, p0, p1), jnp.where(me == 2, p2, p3)))
         pa, pb, v = merge(k + 1, v01, v23, gs[0] + gs[1], gs[2] + gs[3])
-        keep(k + 1, jnp.where(me < 2, pa, pb))
-        return v
-
-    with jax.named_scope("cross_y"):
-        v = four(1, 1, v, v_b, g_b)
-    with jax.named_scope("cross_z"):
-        v = four(2, 3, v, v_c, g_c)
-    with jax.named_scope("cross_x"):
-        share(3, g_d, send_g, recv_g, wait=True)
-        four(3, 5, v, v_d, g_d)
+
+        def keep():
+            partner[:, (k - 1) * RANK : k * RANK] = jnp.where(
+                me < 2, jnp.where(me == 0, p0, p1), jnp.where(me == 2, p2, p3)
+            )
+            partner[:, k * RANK : (k + 1) * RANK] = jnp.where(me < 2, pa, pb)
+
+        return v, keep
+
+    hand = remote(
+        partner,
+        partner,
+        part_sem.at[0],
+        part_sem.at[1],
+        {"leaf": lax.axis_index("leaf"), "sub": lax.axis_index("sub") // 2 * 2},
+    )
+    with jax.named_scope("cross"):
+
+        @pl.when(core == 1)
+        def _():
+            def first():
+                share(2, g_c, send_g, recv_g, wait=True)
+                xsum = (g_c[0, :32].astype(F32) + g_c[1, :32].astype(F32)) + (
+                    g_c[2, :32].astype(F32) + g_c[3, :32].astype(F32)
+                )
+                g_d[group(3)[1]] = xsum.astype(BF16)
+                share(3, g_d, send_g, recv_g)
+                near_update()
+
+            def last():
+                keep()
+                share(3, g_d, send_g, recv_g, wait=True)
+
+            v = merge(0, v_a[0], v_a[1], g_a[0], g_a[1])[2]
+            v, keep = four(1, 1, v, v_b, g_b, first)
+            v, keep = four(2, 3, v, v_c, g_c, keep)
+            v, keep = four(3, 5, v, v_d, g_d, last)
+            keep()
+            hand.start()
+            hand.wait_send()
+
+        @pl.when(core == 0)
+        def _():
+            near_update()
+            hand.wait_recv()
+
     with jax.named_scope("finish"):
         for c in range(16):
             at = slice(c * LEAF, (c + 1) * LEAF)
             done = field[:, at] - dot(
-                partner[:, : CROSS * RANK], left[LOCAL:, :, at].reshape(CROSS * RANK, LEAF)
+                partner[:, : 6 * RANK], left[LOCAL + 1 :, :, at].reshape(6 * RANK, LEAF)
             )
             x[at, :] = jnp.concatenate([done, done], axis=0).T
         back_copy.wait()
@@ -609,12 +634,13 @@
 
 def body(vectors, row_counts, tree_slot, leaf_inverse, left_basis, right_basis):
     anywhere = pl.BlockSpec(memory_space=pl.ANY)
+    outside = pl.BlockSpec(memory_space=pltpu.HBM)
     dma = pltpu.SemaphoreType.DMA
     blocks = pltpu.VMEM((DEV * 5, 4, 128), BF16)
     return pl.pallas_call(
         kernel,
         out_shape=jax.ShapeDtypeStruct((VECS, SLOTS), BF16),
-        in_specs=[SMEM] + [anywhere] * 6,
+        in_specs=[SMEM] + [outside] * 6,
         out_specs=anywhere,
         scratch_shapes=[
             pltpu.VMEM((DEV, 128), I32),
@@ -656,21 +682,34 @@
             pltpu.VMEM((16, VECS, LOCAL * RANK), BF16),
             dma((6,)),
             dma((2,)),
+            dma((2,)),
             dma((4,)),
             dma((2,)),
             dma((16,)),
             dma((16,)),
-            dma((4, 2)),
             dma((4,)),
-            dma((4, 2)),
+            dma((4,)),
+            dma((4,)),
             dma((4,)),
         ],
-        compiler_params=pltpu.CompilerParams(collective_id=0, has_side_effects=True),
+        compiler_params=pltpu.CompilerParams(
+            collective_id=0, has_side_effects=True, vmem_limit_bytes=36 * 2**20
+        ),
         name="apply",
     )(
-        row_counts,
-        jnp.asarray(np.repeat(CODES[:, None], 128, 1)),
-        tree_slot.reshape(40, 128), vectors, leaf_inverse, left_basis, right_basis)
+        *(
+            pltpu.with_memory_space_constraint(value, pltpu.HBM)
+            for value in (
+                row_counts,
+                jnp.asarray(np.repeat(CODES[:, None], 128, 1)),
+                tree_slot.reshape(40, 128),
+                vectors,
+                leaf_inverse,
+                left_basis,
+                right_basis,
+            )
+        ),
+    )
 
 
 def solution(mesh):

time: 60.6 us -> 58.2 us (0.960)
  Pallas kernels: 58.5 us -> 57.3 us
  local copies, waits for them, and re-layouts: 1.97 us -> 0.84 us
    pallas_call x1, Pallas kernels: 58.5 us -> 57.3 us  [body(): pl.pallas_call(kernel, out_shape=jax.ShapeDtypeStruct((VECS, SLOTS), BF16...]
    unnamed x1, local copies, waits for them, and re-layouts: 1.97 us -> 0.84 us
where the time goes in v4:
time: 58.2 us; the launch traced here: 58.1 us
  Pallas kernels  57.3 us (98%)
  local copies, waits for them, and re-layouts  0.84 us (1%)
    pallas_call x1, Pallas kernels, body(): pl.pallas_call(kernel, out_shape=jax.ShapeDtypeStruct((VECS, SLOTS), BF16...  57.3 us

profile of v4, /device:TPU:1, one launch (start us, length us, event | category | flops | bytes accessed | tf_op | source)
XLA Modules:
  0.0 58.1 jit_solution(2256077383934990559)
XLA Ops:
  0.0 57.3 %apply.1 = bf16[64,5120]{1,0:T(8,128)(2,1)S(1)} custom-call(s32[128]{0:T(128)} %counts.1, s32[128,128]{1,0:T(8,128)} %constant.2.clone.codes_h, s32[40,128]{1,0:T(8,128)} %bitcast.1, bf16[64,5120]{1,0:T(8,128)(2,1)} %vec_h.1, bf16[16,256,256]{2,1,0:T(8,128)(2,1)} %inverse_h.1, bf16[11,32,4096]{2,1,0:T(8,128)(2,1)} %left_h.1, bf16[11,32,4096]{2,1,0:T(8,128)(2,1)} %right_h.1), custom_call_target="tpu_custom_call" | custom-call | tf_op jit(solution)/shard_map/apply/pallas_call | solution.py:640
  57.3 0.8 %copy.9 = bf16[64,5120]{1,0:T(8,128)(2,1)} copy(bf16[64,5120]{1,0:T(8,128)(2,1)S(1)} %apply.1) | data formatting | bytes 1310720

commit v5 on v4

--- a/solution.py
+++ b/solution.py
@@ -256,11 +256,10 @@
     inverse_h,
     left_h,
     right_h,
-    out_h,
+    out,
     codes,
     slots_ref,
     vec,
-    out,
     inverse,
     left,
     right,
@@ -617,23 +616,13 @@
             pull_slots(2 * c + 3)
             return carry
 
-        stores = []
-        for part in range(4):
-            lax.fori_loop(5 * part, 5 * part + 5 - part // 3, next_slots, 0)
-            if part == 3:
-                push(38)
-                push(39)
-            at = pl.ds(part * 1280, 1280)
-            store = pltpu.make_async_copy(out.at[:, at], out_h.at[:, at], load_sem.at[part])
-            store.start()
-            stores.append(store)
-        for store in stores:
-            store.wait()
+        lax.fori_loop(0, 19, next_slots, 0)
+        push(38)
+        push(39)
         sent(src2, send_sem.at[1])
 
 
 def body(vectors, row_counts, tree_slot, leaf_inverse, left_basis, right_basis):
-    anywhere = pl.BlockSpec(memory_space=pl.ANY)
     outside = pl.BlockSpec(memory_space=pltpu.HBM)
     dma = pltpu.SemaphoreType.DMA
     blocks = pltpu.VMEM((DEV * 5, 4, 128), BF16)
@@ -641,11 +630,10 @@
         kernel,
         out_shape=jax.ShapeDtypeStruct((VECS, SLOTS), BF16),
         in_specs=[SMEM] + [outside] * 6,
-        out_specs=anywhere,
+        out_specs=VMEM,
         scratch_shapes=[
             pltpu.VMEM((DEV, 128), I32),
             pltpu.VMEM((40, 128), I32),
-            pltpu.VMEM((VECS, SLOTS), BF16),
             pltpu.VMEM((VECS, SLOTS), BF16),
             pltpu.VMEM(leaf_inverse.shape, BF16),
             pltpu.VMEM(left_basis.shape, BF16),

time: 58.2 us -> 58.1 us (level)
  no operation moved by 1% of the time
where the time goes in v5:
time: 58.1 us; the launch traced here: 58 us
  Pallas kernels  57.2 us (98%)
  local copies, waits for them, and re-layouts  0.84 us (1%)
    pallas_call x1, Pallas kernels, body(): pl.pallas_call(kernel, out_shape=jax.ShapeDtypeStruct((VECS, SLOTS), BF16...  57.2 us

profile of v5, /device:TPU:1, one launch (start us, length us, event | category | flops | bytes accessed | tf_op | source)
XLA Modules:
  0.0 58.0 jit_solution(7728805511326154788)
XLA Ops:
  0.0 57.2 %apply.1 = bf16[64,5120]{1,0:T(8,128)(2,1)S(1)} custom-call(s32[128]{0:T(128)} %counts.1, s32[128,128]{1,0:T(8,128)} %constant.2.clone.codes_h, s32[40,128]{1,0:T(8,128)} %bitcast.1, bf16[64,5120]{1,0:T(8,128)(2,1)} %vec_h.1, bf16[16,256,256]{2,1,0:T(8,128)(2,1)} %inverse_h.1, bf16[11,32,4096]{2,1,0:T(8,128)(2,1)} %left_h.1, bf16[11,32,4096]{2,1,0:T(8,128)(2,1)} %right_h.1), custom_call_target="tpu_custom_call" | custom-call | tf_op jit(solution)/shard_map/apply/pallas_call | solution.py:629
  57.2 0.8 %copy.9 = bf16[64,5120]{1,0:T(8,128)(2,1)} copy(bf16[64,5120]{1,0:T(8,128)(2,1)S(1)} %apply.1) | data formatting | bytes 1310720
